TPU v7x, 256 devices: a whole 4x4x8 slice. The times are simulated.
256 devices in a mesh: section: 8 (over y, x_hi), fsdp: 32 (over x_lo, z, core).
Axes of the slice: x: 4 (x_hi: 2, x_lo: 2; x = x_hi * 2 + x_lo), y: 4, z: 8, core: 2. Of those that a mesh axis runs over, the one named last changes fastest.
Arguments:
- codes: int32 [8, 8192, 512], P('section', 'fsdp'), may hold values from 0 to 15
- scale_codes: int32 [8, 8192, 8], P('section', 'fsdp'), may hold values from 0 to 255
- second_scales: float32 [8, 256], P('section', 'fsdp'), may hold values from 0.015 to 0.09
- gains: bfloat16 [8, 8192], P('section'), may hold values from 0.5 to 1.5
- down_adapter: bfloat16 [8, 8192, 64], P('section'), may hold values from -0.0625 to 0.0625
- up_projection_weight: bfloat16 [8, 512, 64], P('section'), may hold values from -0.75 to 0.75
- hidden_in: bfloat16 [4096, 8192], P('fsdp'), may hold values from -6 to 6
- cotangent: bfloat16 [4096, 8192], P('fsdp'), may hold values from -6 to 6
Outputs:
- input_grad: bfloat16 [8, 4096, 8192], P('section', 'fsdp')
- grad_down: float32 [8, 8192, 64], P('section', 'fsdp')
- grad_up: float32 [8, 512, 64], P('section', 'fsdp')
All inputs are finite; a program needn't handle non-finite values.
Results may differ from a plain program's by a relative error of at most 0.025.
Values may be sent and summed in bfloat16 or wider, within the bound.
A program may use at most 128 MiB of HBM per device.

v0:
```python
import jax
import jax.numpy as jnp
from jax import lax
from jax.sharding import PartitionSpec as P

HEAD = 128
GROUP = 8
KV_HEADS = 4
BLOCK = 64
SROWS = 32
MICRO = 4


NF4_TABLE = (
    -1.0,
    -0.6961928009986877,
    -0.5250730514526367,
    -0.39491748809814453,
    -0.28444138169288635,
    -0.18477343022823334,
    -0.09105003625154495,
    0.0,
    0.07958029955625534,
    0.16093020141124725,
    0.24611230194568634,
    0.33791524171066284,
    0.44070982933044434,
    0.5626170039176941,
    0.7229568362236023,
    1.0,
)
adapter_scale = 0.5
epsilon = 1e-05


def from_behind(block, axis, distance):
    devices = range(lax.axis_size(axis))
    route = [(i - distance, i) for i in devices if i - distance in devices]
    return lax.ppermute(block, axis, route)


def cut_along(shard, dim, length):
    lengths = shard.shape
    tiles = shard.reshape(*lengths[:dim], length, lengths[dim] // length, *lengths[dim + 1 :])
    return jnp.moveaxis(tiles, dim, 0)


def sent_and_summed(shard, axis, dim):
    tiles = cut_along(shard, dim, lax.axis_size(axis))
    arrived = lax.all_to_all(tiles, axis, split_axis=0, concat_axis=0, tiled=True)
    return arrived.astype(jnp.float32).sum(axis=0)


def dequantize_shard(codes, scale_codes, second_scales):
    value_rows = jnp.zeros(codes.shape, jnp.float32)
    for entry in range(16):
        value_rows = jnp.where(codes == entry, jnp.float32(NF4_TABLE[entry]), value_rows)
    outer = jnp.repeat(second_scales, SROWS)
    block = outer[:, None] * (scale_codes.astype(jnp.float32) + 1.0) / 256.0
    scaled = value_rows.reshape(codes.shape[0], scale_codes.shape[1], BLOCK) * block[:, :, None]
    return scaled.reshape(codes.shape).astype(jnp.bfloat16)


def spread_heads(value_rows, width):
    count = value_rows.shape[0]
    heads = value_rows.reshape(count, KV_HEADS, 1, HEAD)
    wide = jnp.broadcast_to(heads, (count, KV_HEADS, GROUP, HEAD)).reshape(
        count, KV_HEADS * GROUP * HEAD
    )
    filler = jnp.zeros((count, width - KV_HEADS * GROUP * HEAD), value_rows.dtype)
    return jnp.concatenate([wide, filler], axis=1)


def collapse_heads(grads):
    count = grads.shape[0]
    part = grads[:, : KV_HEADS * GROUP * HEAD].reshape(count, KV_HEADS, GROUP, HEAD)
    return jnp.sum(part, axis=2).reshape(count, KV_HEADS * HEAD)


def shards(
    codes,
    scale_codes,
    second_scales,
    gains,
    down_adapter,
    up_projection_weight,
    hidden_in,
    cotangent,
):
    section = lax.axis_index("section")
    sections = lax.axis_size("section")
    shard = dequantize_shard(codes[0], scale_codes[0], second_scales[0])
    weight = lax.all_gather(shard, "fsdp", axis=0, tiled=True)
    gain = gains[0].astype(jnp.float32)
    down = down_adapter[0]
    raised_output = up_projection_weight[0]
    width = hidden_in.shape[1]
    rows = hidden_in.shape[0] // MICRO
    ticks = MICRO + sections - 1
    rank = down.shape[1]
    value_width = raised_output.shape[0]

    def forward_tick(carry, tick):
        state, saved_in, saved_normed, saved_low = carry
        incoming = from_behind(state, "section", 1)
        position = tick - section
        active = (position >= 0) & (position < MICRO)
        slot = jnp.clip(position, 0, MICRO - 1)
        first = lax.dynamic_slice_in_dim(hidden_in, slot * rows, rows, 0)
        current_in = jnp.where(section == 0, first, incoming)

        def forward_compute(operands):
            current_in, saved_in, saved_normed, saved_low = operands
            current = current_in.astype(jnp.float32)
            root_mean = jnp.sqrt(jnp.mean(current * current, axis=1, keepdims=True) + epsilon)
            normalized_input = (current / root_mean * gain).astype(jnp.bfloat16)
            narrow_product = jnp.dot(
                normalized_input, down, preferred_element_type=jnp.float32
            ).astype(jnp.bfloat16)
            value_rows = jnp.dot(
                normalized_input, weight, preferred_element_type=jnp.float32
            ) + adapter_scale * jnp.dot(
                narrow_product, raised_output.T, preferred_element_type=jnp.float32
            )
            result = (current + spread_heads(value_rows, width)).astype(jnp.bfloat16)
            return (
                result,
                lax.dynamic_update_index_in_dim(saved_in, current_in, slot, 0),
                lax.dynamic_update_index_in_dim(saved_normed, normalized_input, slot, 0),
                lax.dynamic_update_index_in_dim(saved_low, narrow_product, slot, 0),
            )

        def forward_pause(operands):
            return operands

        updated = lax.cond(
            active, forward_compute, forward_pause, (current_in, saved_in, saved_normed, saved_low)
        )
        return (updated, None)

    start = (
        jnp.zeros((rows, width), jnp.bfloat16),
        jnp.zeros((MICRO, rows, width), jnp.bfloat16),
        jnp.zeros((MICRO, rows, width), jnp.bfloat16),
        jnp.zeros((MICRO, rows, rank), jnp.bfloat16),
    )
    finished, _ = lax.scan(forward_tick, start, jnp.arange(ticks, dtype=jnp.int32))
    last_state, saved_in, saved_normed, saved_low = finished

    def backward_tick(carry, tick):
        state, saved_grad, saved_direction, saved_lowgrad = carry
        incoming = from_behind(state, "section", -1)
        position = tick - (sections - 1 - section)
        active = (position >= 0) & (position < MICRO)
        slot = jnp.clip(position, 0, MICRO - 1)
        final = lax.dynamic_slice_in_dim(cotangent, slot * rows, rows, 0)
        grad_in = jnp.where(section == sections - 1, final, incoming)

        def backward_compute(operands):
            grad_in, saved_grad, saved_direction, saved_lowgrad = operands
            current = lax.dynamic_index_in_dim(saved_in, slot, 0, keepdims=False).astype(
                jnp.float32
            )
            root_mean = jnp.sqrt(jnp.mean(current * current, axis=1, keepdims=True) + epsilon)
            unit = current / root_mean
            incoming_grad = grad_in.astype(jnp.float32)
            descent_vector = collapse_heads(incoming_grad).astype(jnp.bfloat16)
            narrow_gradient = (
                adapter_scale
                * jnp.dot(descent_vector, raised_output, preferred_element_type=jnp.float32)
            ).astype(jnp.bfloat16)
            normed_grad = jnp.dot(
                descent_vector, weight.T, preferred_element_type=jnp.float32
            ) + jnp.dot(narrow_gradient, down.T, preferred_element_type=jnp.float32)
            scaled = normed_grad * gain
            hidden_grad = (
                scaled - unit * jnp.mean(scaled * unit, axis=1, keepdims=True)
            ) / root_mean
            result = (incoming_grad + hidden_grad).astype(jnp.bfloat16)
            return (
                result,
                lax.dynamic_update_index_in_dim(saved_grad, result, slot, 0),
                lax.dynamic_update_index_in_dim(saved_direction, descent_vector, slot, 0),
                lax.dynamic_update_index_in_dim(saved_lowgrad, narrow_gradient, slot, 0),
            )

        def backward_pause(operands):
            return operands

        updated = lax.cond(
            active,
            backward_compute,
            backward_pause,
            (grad_in, saved_grad, saved_direction, saved_lowgrad),
        )
        return (updated, None)

    start_back = (
        jnp.zeros((rows, width), jnp.bfloat16),
        jnp.zeros((MICRO, rows, width), jnp.bfloat16),
        jnp.zeros((MICRO, rows, value_width), jnp.bfloat16),
        jnp.zeros((MICRO, rows, rank), jnp.bfloat16),
    )
    finished_back, _ = lax.scan(backward_tick, start_back, jnp.arange(ticks, dtype=jnp.int32))
    _, saved_grad, saved_direction, saved_lowgrad = finished_back
    tokens_here = MICRO * rows
    directions = saved_direction.reshape(tokens_here, value_width)
    lowranks = saved_low.reshape(tokens_here, rank)
    normeds = saved_normed.reshape(tokens_here, width)
    low_grads = saved_lowgrad.reshape(tokens_here, rank)
    contract = (((0,), (0,)), ((), ()))
    up_weight_gradient = adapter_scale * lax.dot_general(
        directions, lowranks, contract, preferred_element_type=jnp.float32
    )
    down_grad = lax.dot_general(normeds, low_grads, contract, preferred_element_type=jnp.float32)
    down_part, up_part = (
        sent_and_summed(down_grad.astype(jnp.bfloat16), "fsdp", 0),
        sent_and_summed(up_weight_gradient.astype(jnp.bfloat16), "fsdp", 0),
    )
    input_grad = saved_grad.reshape(1, tokens_here, width)
    return (input_grad, down_part[None], up_part[None])


def solution(mesh):
    return jax.shard_map(
        shards,
        mesh=mesh,
        in_specs=(
            P("section", "fsdp", None),
            P("section", "fsdp", None),
            P("section", "fsdp"),
            P("section", None),
            P("section", None, None),
            P("section", None, None),
            P("fsdp", None),
            P("fsdp", None),
        ),
        out_specs=(
            P("section", "fsdp", None),
            P("section", "fsdp", None),
            P("section", "fsdp", None),
        ),
        check_vma=False,
    )
```

profile of v0, /device:TPU:32, one launch (start us, length us, event | category | flops | bytes accessed | tf_op | source)
XLA Modules:
  0.0 660.1 jit_solution(1380995913632222256)
XLA Ops:
  13.4 90.0 %all-gather.2.cloned.1.call-done = bf16[8192,512]{0,1:T(8,128)(2,1)} async-done(((bf16[256,512]{0,1:T(8,128)(2,1)}), bf16[8192,512]{0,1:T(8,128)(2,1)}) %all-gather.2.cloned.1.call-update) | async-done | bytes 8388624 | tf_op jit(solution)/shard_map/all_gather | solution.py:93
  103.4 12.0 %copy.54 = bf16[8192,512]{1,0:T(8,128)(2,1)} copy(bf16[8192,512]{0,1:T(8,128)(2,1)} %all-gather.2.cloned.1.call-done) | data formatting | bytes 16777216 | tf_op jit(solution)/shard_map/while | solution.py:204
  117.2 215.5 %while.35 = (s32[]{:T(128)}, bf16[32,8192]{1,0:T(8,128)(2,1)S(1)}, bf16[4,32,8192]{2,1,0:T(8,128)(2,1)S(1)}, bf16[4,32,8192]{2,1,0:T(8,128)(2,1)}, bf16[4,32,64]...) while((s32[]{:T(128)}, bf16[32,8192]{1,0:T(8,128)(2,1)S(1)}, ...), condition=%wide.region_4.5_spmd, body=%wide.region_0.4_spmd.sunk | while | flops 309102624 | bytes 25221160 | solution.py:147
  123.0 10.3 %collective-permute-done = bf16[32,8192]{1,0:T(8,128)(2,1)S(1)} collective-permute-done((bf16[32,8192]{1,0:T(8,128)(2,1)S(1)}, bf16[32,8192]{1,0:T(8,128)(2,1)S(1)}, u32[]{:S(2)}, u32[]{:S(2)}) %collective-permute-start) | collective-permute-done | bytes 524320 | tf_op jit(solution)/shard_map/while/body/eval_jaxpr/ppermute | solution.py:39
  144.8 9.7 %collective-permute-done = bf16[32,8192]{1,0:T(8,128)(2,1)S(1)} collective-permute-done((bf16[32,8192]{1,0:T(8,128)(2,1)S(1)}, bf16[32,8192]{1,0:T(8,128)(2,1)S(1)}, u32[]{:S(2)}, u32[]{:S(2)}) %collective-permute-start) | collective-permute-done | bytes 524320 | tf_op jit(solution)/shard_map/while/body/eval_jaxpr/ppermute | solution.py:39
  170.6 8.8 %collective-permute-done = bf16[32,8192]{1,0:T(8,128)(2,1)S(1)} collective-permute-done((bf16[32,8192]{1,0:T(8,128)(2,1)S(1)}, bf16[32,8192]{1,0:T(8,128)(2,1)S(1)}, u32[]{:S(2)}, u32[]{:S(2)}) %collective-permute-start) | collective-permute-done | bytes 524320 | tf_op jit(solution)/shard_map/while/body/eval_jaxpr/ppermute | solution.py:39
  227.9 13.6 %collective-permute-start = (bf16[32,8192]{1,0:T(8,128)(2,1)S(1)}, bf16[32,8192]{1,0:T(8,128)(2,1)S(1)}, u32[]{:S(2)}, u32[]{:S(2)}) collective-permute-start(bf16[32,8192]{1,0:T(8,128)(2,1)S(1)} %get-tuple-element.701), channel_id=1, source_target_pairs={{0,32},{32,64},{64,96},{96,128},{128,160},{160,192},{192,224},{1,3... | collective-permute-start | bytes 1572872 | tf_op jit(solution)/shard_map/while/body/eval_jaxpr/ppermute | solution.py:39
  264.2 14.5 %collective-permute-start = (bf16[32,8192]{1,0:T(8,128)(2,1)S(1)}, bf16[32,8192]{1,0:T(8,128)(2,1)S(1)}, u32[]{:S(2)}, u32[]{:S(2)}) collective-permute-start(bf16[32,8192]{1,0:T(8,128)(2,1)S(1)} %get-tuple-element.701), channel_id=1, source_target_pairs={{0,32},{32,64},{64,96},{96,128},{128,160},{160,192},{192,224},{1,3... | collective-permute-start | bytes 1572872 | tf_op jit(solution)/shard_map/while/body/eval_jaxpr/ppermute | solution.py:39
  301.2 9.0 %collective-permute-start = (bf16[32,8192]{1,0:T(8,128)(2,1)S(1)}, bf16[32,8192]{1,0:T(8,128)(2,1)S(1)}, u32[]{:S(2)}, u32[]{:S(2)}) collective-permute-start(bf16[32,8192]{1,0:T(8,128)(2,1)S(1)} %get-tuple-element.701), channel_id=1, source_target_pairs={{0,32},{32,64},{64,96},{96,128},{128,160},{160,192},{192,224},{1,3... | collective-permute-start | bytes 1572872 | tf_op jit(solution)/shard_map/while/body/eval_jaxpr/ppermute | solution.py:39
  334.3 271.0 %while.36 = (s32[]{:T(128)}, bf16[32,8192]{1,0:T(8,128)(2,1)S(1)}, bf16[4,32,8192]{2,1,0:T(8,128)(2,1)}, bf16[4,32,512]{2,1,0:T(8,128)(2,1)S(1)}, bf16[4,32,64]{...) while((s32[]{:T(128)}, bf16[32,8192]{1,0:T(8,128)(2,1)S(1)}, ...), condition=%wide.region_11.12_spmd, body=%wide.region_5.11_spmd.sunk | while | flops 309186592 | bytes 28268232 | solution.py:204
  336.8 19.6 %collective-permute-done.1 = bf16[32,8192]{1,0:T(8,128)(2,1)S(1)} collective-permute-done((bf16[32,8192]{1,0:T(8,128)(2,1)S(1)}, bf16[32,8192]{1,0:T(8,128)(2,1)S(1)}, u32[]{:S(2)}, u32[]{:S(2)}) %collective-permute-start.1) | collective-permute-done | bytes 524320 | tf_op jit(solution)/shard_map/while/body/eval_jaxpr/ppermute | solution.py:39
  360.2 11.3 %collective-permute-done.1 = bf16[32,8192]{1,0:T(8,128)(2,1)S(1)} collective-permute-done((bf16[32,8192]{1,0:T(8,128)(2,1)S(1)}, bf16[32,8192]{1,0:T(8,128)(2,1)S(1)}, u32[]{:S(2)}, u32[]{:S(2)}) %collective-permute-start.1) | collective-permute-done | bytes 524320 | tf_op jit(solution)/shard_map/while/body/eval_jaxpr/ppermute | solution.py:39
  375.3 22.6 %collective-permute-done.1 = bf16[32,8192]{1,0:T(8,128)(2,1)S(1)} collective-permute-done((bf16[32,8192]{1,0:T(8,128)(2,1)S(1)}, bf16[32,8192]{1,0:T(8,128)(2,1)S(1)}, u32[]{:S(2)}, u32[]{:S(2)}) %collective-permute-start.1) | collective-permute-done | bytes 524320 | tf_op jit(solution)/shard_map/while/body/eval_jaxpr/ppermute | solution.py:39
  401.6 14.8 %collective-permute-done.1 = bf16[32,8192]{1,0:T(8,128)(2,1)S(1)} collective-permute-done((bf16[32,8192]{1,0:T(8,128)(2,1)S(1)}, bf16[32,8192]{1,0:T(8,128)(2,1)S(1)}, u32[]{:S(2)}, u32[]{:S(2)}) %collective-permute-start.1) | collective-permute-done | bytes 524320 | tf_op jit(solution)/shard_map/while/body/eval_jaxpr/ppermute | solution.py:39
  420.1 19.9 %collective-permute-done.1 = bf16[32,8192]{1,0:T(8,128)(2,1)S(1)} collective-permute-done((bf16[32,8192]{1,0:T(8,128)(2,1)S(1)}, bf16[32,8192]{1,0:T(8,128)(2,1)S(1)}, u32[]{:S(2)}, u32[]{:S(2)}) %collective-permute-start.1) | collective-permute-done | bytes 524320 | tf_op jit(solution)/shard_map/while/body/eval_jaxpr/ppermute | solution.py:39
  443.8 17.1 %collective-permute-done.1 = bf16[32,8192]{1,0:T(8,128)(2,1)S(1)} collective-permute-done((bf16[32,8192]{1,0:T(8,128)(2,1)S(1)}, bf16[32,8192]{1,0:T(8,128)(2,1)S(1)}, u32[]{:S(2)}, u32[]{:S(2)}) %collective-permute-start.1) | collective-permute-done | bytes 524320 | tf_op jit(solution)/shard_map/while/body/eval_jaxpr/ppermute | solution.py:39
  464.7 10.0 %collective-permute-done.1 = bf16[32,8192]{1,0:T(8,128)(2,1)S(1)} collective-permute-done((bf16[32,8192]{1,0:T(8,128)(2,1)S(1)}, bf16[32,8192]{1,0:T(8,128)(2,1)S(1)}, u32[]{:S(2)}, u32[]{:S(2)}) %collective-permute-start.1) | collective-permute-done | bytes 524320 | tf_op jit(solution)/shard_map/while/body/eval_jaxpr/ppermute | solution.py:39
  478.5 43.8 %collective-permute-done.1 = bf16[32,8192]{1,0:T(8,128)(2,1)S(1)} collective-permute-done((bf16[32,8192]{1,0:T(8,128)(2,1)S(1)}, bf16[32,8192]{1,0:T(8,128)(2,1)S(1)}, u32[]{:S(2)}, u32[]{:S(2)}) %collective-permute-start.1) | collective-permute-done | bytes 524320 | tf_op jit(solution)/shard_map/while/body/eval_jaxpr/ppermute | solution.py:39
  523.5 8.8 %conditional.5 = ((bf16[32,8192]{1,0:T(8,128)(2,1)S(1)}, bf16[4,32,8192]{2,1,0:T(8,128)(2,1)}, bf16[4,32,512]{2,1,0:T(8,128)(2,1)S(1)}, bf16[4,32,64]{2,1,0:T(8,128)(2,1)S(1)})) conditional(s32[]{:T(128)} %convert_element_type.131, (bf16[32,8192]{1,0:T(8,128)(2,1)S(1)}, bf16[4,32,8192]{2,1,0:T(8,128)(2,1)}, bf16[4,32,512]{2,1,0:T(8,128)(2,1)S(1)}, ...), branch_computations={%region_6.6_spmd, %region_7.10_spmd} | conditional | flops 308924448 | bytes 24597758 | solution.py:190
  534.9 10.9 %collective-permute-done.1 = bf16[32,8192]{1,0:T(8,128)(2,1)S(1)} collective-permute-done((bf16[32,8192]{1,0:T(8,128)(2,1)S(1)}, bf16[32,8192]{1,0:T(8,128)(2,1)S(1)}, u32[]{:S(2)}, u32[]{:S(2)}) %collective-permute-start.1) | collective-permute-done | bytes 524320 | tf_op jit(solution)/shard_map/while/body/eval_jaxpr/ppermute | solution.py:39
  558.3 11.5 %collective-permute-done.1 = bf16[32,8192]{1,0:T(8,128)(2,1)S(1)} collective-permute-done((bf16[32,8192]{1,0:T(8,128)(2,1)S(1)}, bf16[32,8192]{1,0:T(8,128)(2,1)S(1)}, u32[]{:S(2)}, u32[]{:S(2)}) %collective-permute-start.1) | collective-permute-done | bytes 524320 | tf_op jit(solution)/shard_map/while/body/eval_jaxpr/ppermute | solution.py:39
  571.0 8.8 %conditional.5 = ((bf16[32,8192]{1,0:T(8,128)(2,1)S(1)}, bf16[4,32,8192]{2,1,0:T(8,128)(2,1)}, bf16[4,32,512]{2,1,0:T(8,128)(2,1)S(1)}, bf16[4,32,64]{2,1,0:T(8,128)(2,1)S(1)})) conditional(s32[]{:T(128)} %convert_element_type.131, (bf16[32,8192]{1,0:T(8,128)(2,1)S(1)}, bf16[4,32,8192]{2,1,0:T(8,128)(2,1)}, bf16[4,32,512]{2,1,0:T(8,128)(2,1)S(1)}, ...), branch_computations={%region_6.6_spmd, %region_7.10_spmd} | conditional | flops 308924448 | bytes 24597758 | solution.py:190
  582.4 12.9 %collective-permute-done.1 = bf16[32,8192]{1,0:T(8,128)(2,1)S(1)} collective-permute-done((bf16[32,8192]{1,0:T(8,128)(2,1)S(1)}, bf16[32,8192]{1,0:T(8,128)(2,1)S(1)}, u32[]{:S(2)}, u32[]{:S(2)}) %collective-permute-start.1) | collective-permute-done | bytes 524320 | tf_op jit(solution)/shard_map/while/body/eval_jaxpr/ppermute | solution.py:39
  624.2 28.3 %all-to-all-done = bf16[32,256,64]{1,2,0:T(8,128)(2,1)S(1)} async-done(((bf16[32,256,64]{1,2,0:T(8,128)(2,1)}), bf16[32,256,64]{1,2,0:T(8,128)(2,1)S(1)}, u32[]{:S(2)}, u32[]{:S(2)}) %all-to-all-start) | async-done | bytes 1048608 | tf_op jit(solution)/shard_map/all_to_all | solution.py:50
  (236 shorter events, 287.8 us)
Async XLA Ops:
  7.2 96.2 %all-gather.2.cloned.1.call-start = ((), (), s32[]{:S(2)}) async-start(), calls=%async_computation.2 | async-start | bytes 8650752 | tf_op jit(solution)/shard_map/all_gather | solution.py:93
  117.2 16.1 %collective-permute-start = (bf16[32,8192]{1,0:T(8,128)(2,1)S(1)}, bf16[32,8192]{1,0:T(8,128)(2,1)S(1)}, u32[]{:S(2)}, u32[]{:S(2)}) collective-permute-start(bf16[32,8192]{1,0:T(8,128)(2,1)S(1)} %get-tuple-element.701), channel_id=1, source_target_pairs={{0,32},{32,64},{64,96},{96,128},{128,160},{160,192},{192,224},{1,3... | collective-permute-start | bytes 1572872 | tf_op jit(solution)/shard_map/while/body/eval_jaxpr/ppermute | solution.py:39
  142.2 12.3 %collective-permute-start = (bf16[32,8192]{1,0:T(8,128)(2,1)S(1)}, bf16[32,8192]{1,0:T(8,128)(2,1)S(1)}, u32[]{:S(2)}, u32[]{:S(2)}) collective-permute-start(bf16[32,8192]{1,0:T(8,128)(2,1)S(1)} %get-tuple-element.701), channel_id=1, source_target_pairs={{0,32},{32,64},{64,96},{96,128},{128,160},{160,192},{192,224},{1,3... | collective-permute-start | bytes 1572872 | tf_op jit(solution)/shard_map/while/body/eval_jaxpr/ppermute | solution.py:39
  163.4 16.0 %collective-permute-start = (bf16[32,8192]{1,0:T(8,128)(2,1)S(1)}, bf16[32,8192]{1,0:T(8,128)(2,1)S(1)}, u32[]{:S(2)}, u32[]{:S(2)}) collective-permute-start(bf16[32,8192]{1,0:T(8,128)(2,1)S(1)} %get-tuple-element.701), channel_id=1, source_target_pairs={{0,32},{32,64},{64,96},{96,128},{128,160},{160,192},{192,224},{1,3... | collective-permute-start | bytes 1572872 | tf_op jit(solution)/shard_map/while/body/eval_jaxpr/ppermute | solution.py:39
  188.3 15.2 %collective-permute-start = (bf16[32,8192]{1,0:T(8,128)(2,1)S(1)}, bf16[32,8192]{1,0:T(8,128)(2,1)S(1)}, u32[]{:S(2)}, u32[]{:S(2)}) collective-permute-start(bf16[32,8192]{1,0:T(8,128)(2,1)S(1)} %get-tuple-element.701), channel_id=1, source_target_pairs={{0,32},{32,64},{64,96},{96,128},{128,160},{160,192},{192,224},{1,3... | collective-permute-start | bytes 1572872 | tf_op jit(solution)/shard_map/while/body/eval_jaxpr/ppermute | solution.py:39
  212.3 14.3 %collective-permute-start = (bf16[32,8192]{1,0:T(8,128)(2,1)S(1)}, bf16[32,8192]{1,0:T(8,128)(2,1)S(1)}, u32[]{:S(2)}, u32[]{:S(2)}) collective-permute-start(bf16[32,8192]{1,0:T(8,128)(2,1)S(1)} %get-tuple-element.701), channel_id=1, source_target_pairs={{0,32},{32,64},{64,96},{96,128},{128,160},{160,192},{192,224},{1,3... | collective-permute-start | bytes 1572872 | tf_op jit(solution)/shard_map/while/body/eval_jaxpr/ppermute | solution.py:39
  227.9 21.1 %collective-permute-start = (bf16[32,8192]{1,0:T(8,128)(2,1)S(1)}, bf16[32,8192]{1,0:T(8,128)(2,1)S(1)}, u32[]{:S(2)}, u32[]{:S(2)}) collective-permute-start(bf16[32,8192]{1,0:T(8,128)(2,1)S(1)} %get-tuple-element.701), channel_id=1, source_target_pairs={{0,32},{32,64},{64,96},{96,128},{128,160},{160,192},{192,224},{1,3... | collective-permute-start | bytes 1572872 | tf_op jit(solution)/shard_map/while/body/eval_jaxpr/ppermute | solution.py:39
  250.2 12.8 %collective-permute-start = (bf16[32,8192]{1,0:T(8,128)(2,1)S(1)}, bf16[32,8192]{1,0:T(8,128)(2,1)S(1)}, u32[]{:S(2)}, u32[]{:S(2)}) collective-permute-start(bf16[32,8192]{1,0:T(8,128)(2,1)S(1)} %get-tuple-element.701), channel_id=1, source_target_pairs={{0,32},{32,64},{64,96},{96,128},{128,160},{160,192},{192,224},{1,3... | collective-permute-start | bytes 1572872 | tf_op jit(solution)/shard_map/while/body/eval_jaxpr/ppermute | solution.py:39
  264.2 21.1 %collective-permute-start = (bf16[32,8192]{1,0:T(8,128)(2,1)S(1)}, bf16[32,8192]{1,0:T(8,128)(2,1)S(1)}, u32[]{:S(2)}, u32[]{:S(2)}) collective-permute-start(bf16[32,8192]{1,0:T(8,128)(2,1)S(1)} %get-tuple-element.701), channel_id=1, source_target_pairs={{0,32},{32,64},{64,96},{96,128},{128,160},{160,192},{192,224},{1,3... | collective-permute-start | bytes 1572872 | tf_op jit(solution)/shard_map/while/body/eval_jaxpr/ppermute | solution.py:39
  286.5 13.5 %collective-permute-start = (bf16[32,8192]{1,0:T(8,128)(2,1)S(1)}, bf16[32,8192]{1,0:T(8,128)(2,1)S(1)}, u32[]{:S(2)}, u32[]{:S(2)}) collective-permute-start(bf16[32,8192]{1,0:T(8,128)(2,1)S(1)} %get-tuple-element.701), channel_id=1, source_target_pairs={{0,32},{32,64},{64,96},{96,128},{128,160},{160,192},{192,224},{1,3... | collective-permute-start | bytes 1572872 | tf_op jit(solution)/shard_map/while/body/eval_jaxpr/ppermute | solution.py:39
  301.2 15.6 %collective-permute-start = (bf16[32,8192]{1,0:T(8,128)(2,1)S(1)}, bf16[32,8192]{1,0:T(8,128)(2,1)S(1)}, u32[]{:S(2)}, u32[]{:S(2)}) collective-permute-start(bf16[32,8192]{1,0:T(8,128)(2,1)S(1)} %get-tuple-element.701), channel_id=1, source_target_pairs={{0,32},{32,64},{64,96},{96,128},{128,160},{160,192},{192,224},{1,3... | collective-permute-start | bytes 1572872 | tf_op jit(solution)/shard_map/while/body/eval_jaxpr/ppermute | solution.py:39
  318.0 13.5 %collective-permute-start = (bf16[32,8192]{1,0:T(8,128)(2,1)S(1)}, bf16[32,8192]{1,0:T(8,128)(2,1)S(1)}, u32[]{:S(2)}, u32[]{:S(2)}) collective-permute-start(bf16[32,8192]{1,0:T(8,128)(2,1)S(1)} %get-tuple-element.701), channel_id=1, source_target_pairs={{0,32},{32,64},{64,96},{96,128},{128,160},{160,192},{192,224},{1,3... | collective-permute-start | bytes 1572872 | tf_op jit(solution)/shard_map/while/body/eval_jaxpr/ppermute | solution.py:39
  334.3 22.1 %collective-permute-start.1 = (bf16[32,8192]{1,0:T(8,128)(2,1)S(1)}, bf16[32,8192]{1,0:T(8,128)(2,1)S(1)}, u32[]{:S(2)}, u32[]{:S(2)}) collective-permute-start(bf16[32,8192]{1,0:T(8,128)(2,1)S(1)} %get-tuple-element.759), channel_id=1, source_target_pairs={{32,0},{64,32},{96,64},{128,96},{160,128},{192,160},{224,192},{33,... | collective-permute-start | bytes 1572872 | tf_op jit(solution)/shard_map/while/body/eval_jaxpr/ppermute | solution.py:39
  357.6 13.9 %collective-permute-start.1 = (bf16[32,8192]{1,0:T(8,128)(2,1)S(1)}, bf16[32,8192]{1,0:T(8,128)(2,1)S(1)}, u32[]{:S(2)}, u32[]{:S(2)}) collective-permute-start(bf16[32,8192]{1,0:T(8,128)(2,1)S(1)} %get-tuple-element.759), channel_id=1, source_target_pairs={{32,0},{64,32},{96,64},{128,96},{160,128},{192,160},{224,192},{33,... | collective-permute-start | bytes 1572872 | tf_op jit(solution)/shard_map/while/body/eval_jaxpr/ppermute | solution.py:39
  372.7 25.1 %collective-permute-start.1 = (bf16[32,8192]{1,0:T(8,128)(2,1)S(1)}, bf16[32,8192]{1,0:T(8,128)(2,1)S(1)}, u32[]{:S(2)}, u32[]{:S(2)}) collective-permute-start(bf16[32,8192]{1,0:T(8,128)(2,1)S(1)} %get-tuple-element.759), channel_id=1, source_target_pairs={{32,0},{64,32},{96,64},{128,96},{160,128},{192,160},{224,192},{33,... | collective-permute-start | bytes 1572872 | tf_op jit(solution)/shard_map/while/body/eval_jaxpr/ppermute | solution.py:39
  399.0 17.3 %collective-permute-start.1 = (bf16[32,8192]{1,0:T(8,128)(2,1)S(1)}, bf16[32,8192]{1,0:T(8,128)(2,1)S(1)}, u32[]{:S(2)}, u32[]{:S(2)}) collective-permute-start(bf16[32,8192]{1,0:T(8,128)(2,1)S(1)} %get-tuple-element.759), channel_id=1, source_target_pairs={{32,0},{64,32},{96,64},{128,96},{160,128},{192,160},{224,192},{33,... | collective-permute-start | bytes 1572872 | tf_op jit(solution)/shard_map/while/body/eval_jaxpr/ppermute | solution.py:39
  417.6 22.5 %collective-permute-start.1 = (bf16[32,8192]{1,0:T(8,128)(2,1)S(1)}, bf16[32,8192]{1,0:T(8,128)(2,1)S(1)}, u32[]{:S(2)}, u32[]{:S(2)}) collective-permute-start(bf16[32,8192]{1,0:T(8,128)(2,1)S(1)} %get-tuple-element.759), channel_id=1, source_target_pairs={{32,0},{64,32},{96,64},{128,96},{160,128},{192,160},{224,192},{33,... | collective-permute-start | bytes 1572872 | tf_op jit(solution)/shard_map/while/body/eval_jaxpr/ppermute | solution.py:39
  441.3 19.6 %collective-permute-start.1 = (bf16[32,8192]{1,0:T(8,128)(2,1)S(1)}, bf16[32,8192]{1,0:T(8,128)(2,1)S(1)}, u32[]{:S(2)}, u32[]{:S(2)}) collective-permute-start(bf16[32,8192]{1,0:T(8,128)(2,1)S(1)} %get-tuple-element.759), channel_id=1, source_target_pairs={{32,0},{64,32},{96,64},{128,96},{160,128},{192,160},{224,192},{33,... | collective-permute-start | bytes 1572872 | tf_op jit(solution)/shard_map/while/body/eval_jaxpr/ppermute | solution.py:39
  462.1 12.6 %collective-permute-start.1 = (bf16[32,8192]{1,0:T(8,128)(2,1)S(1)}, bf16[32,8192]{1,0:T(8,128)(2,1)S(1)}, u32[]{:S(2)}, u32[]{:S(2)}) collective-permute-start(bf16[32,8192]{1,0:T(8,128)(2,1)S(1)} %get-tuple-element.759), channel_id=1, source_target_pairs={{32,0},{64,32},{96,64},{128,96},{160,128},{192,160},{224,192},{33,... | collective-permute-start | bytes 1572872 | tf_op jit(solution)/shard_map/while/body/eval_jaxpr/ppermute | solution.py:39
  475.9 46.4 %collective-permute-start.1 = (bf16[32,8192]{1,0:T(8,128)(2,1)S(1)}, bf16[32,8192]{1,0:T(8,128)(2,1)S(1)}, u32[]{:S(2)}, u32[]{:S(2)}) collective-permute-start(bf16[32,8192]{1,0:T(8,128)(2,1)S(1)} %get-tuple-element.759), channel_id=1, source_target_pairs={{32,0},{64,32},{96,64},{128,96},{160,128},{192,160},{224,192},{33,... | collective-permute-start | bytes 1572872 | tf_op jit(solution)/shard_map/while/body/eval_jaxpr/ppermute | solution.py:39
  532.3 13.5 %collective-permute-start.1 = (bf16[32,8192]{1,0:T(8,128)(2,1)S(1)}, bf16[32,8192]{1,0:T(8,128)(2,1)S(1)}, u32[]{:S(2)}, u32[]{:S(2)}) collective-permute-start(bf16[32,8192]{1,0:T(8,128)(2,1)S(1)} %get-tuple-element.759), channel_id=1, source_target_pairs={{32,0},{64,32},{96,64},{128,96},{160,128},{192,160},{224,192},{33,... | collective-permute-start | bytes 1572872 | tf_op jit(solution)/shard_map/while/body/eval_jaxpr/ppermute | solution.py:39
  555.8 14.0 %collective-permute-start.1 = (bf16[32,8192]{1,0:T(8,128)(2,1)S(1)}, bf16[32,8192]{1,0:T(8,128)(2,1)S(1)}, u32[]{:S(2)}, u32[]{:S(2)}) collective-permute-start(bf16[32,8192]{1,0:T(8,128)(2,1)S(1)} %get-tuple-element.759), channel_id=1, source_target_pairs={{32,0},{64,32},{96,64},{128,96},{160,128},{192,160},{224,192},{33,... | collective-permute-start | bytes 1572872 | tf_op jit(solution)/shard_map/while/body/eval_jaxpr/ppermute | solution.py:39
  579.8 15.5 %collective-permute-start.1 = (bf16[32,8192]{1,0:T(8,128)(2,1)S(1)}, bf16[32,8192]{1,0:T(8,128)(2,1)S(1)}, u32[]{:S(2)}, u32[]{:S(2)}) collective-permute-start(bf16[32,8192]{1,0:T(8,128)(2,1)S(1)} %get-tuple-element.759), channel_id=1, source_target_pairs={{32,0},{64,32},{96,64},{128,96},{160,128},{192,160},{224,192},{33,... | collective-permute-start | bytes 1572872 | tf_op jit(solution)/shard_map/while/body/eval_jaxpr/ppermute | solution.py:39
  618.4 34.1 %all-to-all-start = ((bf16[32,256,64]{1,2,0:T(8,128)(2,1)}), bf16[32,256,64]{1,2,0:T(8,128)(2,1)S(1)}, u32[]{:S(2)}, u32[]{:S(2)}) async-start(bf16[32,256,64]{1,2,0:T(8,128)(2,1)} %bitcast.84), calls=%async_computation | async-start | bytes 2097152 | tf_op jit(solution)/shard_map/all_to_all | solution.py:50
  (12 other events, 70.5 us)
Sparse Core Ops, SparseCore 0:
  11.5 91.8 all-gather.1
where the time goes:
time: 663 us; the launch traced here: 660 us
  waiting for transfers between devices  395 us (60%)
  starting transfers between devices  104 us (16%)
  matrix products  54 us (8%)
  other arithmetic  40.8 us (6%)
  local copies, waits for them, and re-layouts  36.4 us (5%)
  loops' own time  16.3 us (2%)
  between operations  14.2 us (2%)
    ppermute x22, waiting for transfers between devices, from_behind(): return lax.ppermute(block, axis, route)  272 us
    ppermute x22, starting transfers between devices, from_behind(): return lax.ppermute(block, axis, route)  94.5 us
    all_gather x1, waiting for transfers between devices, shards(): weight = lax.all_gather(shard, 'fsdp', axis=0, tiled=True)  90 us
    all_to_all x2, waiting for transfers between devices, sent_and_summed(): lax.all_to_all(tiles, axis, split_axis=0, concat_axis=0, tiled=True)  33 us
    dot_general x4, matrix products, backward_compute(): jnp.dot(descent_vector, weight.T, preferred_element_type=jnp.float32)  24.2 us
    dot_general x4, matrix products, forward_compute(): jnp.dot(normalized_input, weight, preferred_element_type=jnp.float32)  20.5 us
  transfers between devices with their start and end apart: 25, of which 25 were waited for; matrix products, arithmetic and copies ran while one was open for 3% of the time, Pallas kernels for 0%

commit v1 on v0

v1 whole, which is shorter than its diff:
```python
import jax
import jax.numpy as jnp
from jax import lax
from jax.experimental import pallas as pl
from jax.experimental.pallas import tpu as pltpu
from jax.sharding import PartitionSpec as P

HEAD = 128
GROUP = 8
KV_HEADS = 4
KVW = KV_HEADS * HEAD
BLOCK = 64
SROWS = 32

NF4_TABLE = (
    -1.0,
    -0.6961928009986877,
    -0.5250730514526367,
    -0.39491748809814453,
    -0.28444138169288635,
    -0.18477343022823334,
    -0.09105003625154495,
    0.0,
    0.07958029955625534,
    0.16093020141124725,
    0.24611230194568634,
    0.33791524171066284,
    0.44070982933044434,
    0.5626170039176941,
    0.7229568362236023,
    1.0,
)
adapter_scale = 0.5
epsilon = 1e-05
F32 = jnp.float32
BF16 = jnp.bfloat16


def dequantize_shard(codes, scale_codes, second_scales):
    value_rows = jnp.zeros(codes.shape, jnp.float32)
    for entry in range(16):
        value_rows = jnp.where(codes == entry, jnp.float32(NF4_TABLE[entry]), value_rows)
    outer = jnp.repeat(second_scales, SROWS)
    block = outer[:, None] * (scale_codes.astype(jnp.float32) + 1.0) / 256.0
    scaled = value_rows.reshape(codes.shape[0], scale_codes.shape[1], BLOCK) * block[:, :, None]
    return scaled.reshape(codes.shape).astype(jnp.bfloat16)


def collapse(rows):
    count = rows.shape[0]
    part = rows[:, : GROUP * KVW].reshape(count, KV_HEADS, GROUP, HEAD)
    return jnp.sum(part, axis=2).reshape(count, KVW)


def spread(rows, width):
    count = rows.shape[0]
    heads = rows.reshape(count, KV_HEADS, 1, HEAD)
    wide = jnp.broadcast_to(heads, (count, KV_HEADS, GROUP, HEAD)).reshape(count, GROUP * KVW)
    return jnp.concatenate([wide, jnp.zeros((count, width - GROUP * KVW), rows.dtype)], axis=1)


def chain_kernel(width, products, mixes, folded, squares, descent, reply):
    layers = products.shape[0]
    folded_hidden = folded[...]
    square_sum = squares[...]
    total = jnp.zeros_like(folded_hidden)
    totals, inverses, values = [], [], []
    for layer in range(layers):
        moved = 2.0 * folded_hidden + GROUP * total
        square = square_sum + jnp.sum(total * moved, axis=1, keepdims=True)
        inverse = 1.0 / jnp.sqrt(square / width + epsilon)
        mixed = products[layer].astype(F32)
        if layer:
            mixed += jnp.dot(total.astype(BF16), mixes[layer], preferred_element_type=F32)
        value = mixed * inverse
        totals.append(total)
        inverses.append(inverse)
        values.append(value)
        total = total + value
    direction = descent[...]
    for layer in reversed(range(layers)):
        inverse = inverses[layer]
        ratio = jnp.sum(direction * values[layer], axis=1, keepdims=True) / width
        slope = ratio * inverse * inverse
        scaled = (direction * inverse).astype(BF16)
        reply[layer, :, :KVW] = scaled
        reply[layer, :, KVW : 2 * KVW] = totals[layer].astype(BF16)
        reply[layer, :, 2 * KVW :] = jnp.broadcast_to(slope, (slope.shape[0], HEAD)).astype(BF16)
        if layer:
            direction = (
                direction
                + lax.dot_general(
                    scaled, mixes[layer], (((1,), (1,)), ((), ())), preferred_element_type=F32
                )
                - (folded_hidden + GROUP * totals[layer]) * slope
            )


def shards(
    codes,
    scale_codes,
    second_scales,
    gains,
    down_adapter,
    up_projection_weight,
    hidden_in,
    cotangent,
):
    section = lax.axis_index("section")
    sections = lax.axis_size("section")
    place = lax.axis_index("fsdp")
    places = lax.axis_size("fsdp")
    gain = gains[0].astype(F32)
    down = down_adapter[0]
    raised = up_projection_weight[0]
    tokens, width = hidden_in.shape
    rank = down.shape[1]
    own_rows = codes.shape[1]
    own = tokens // sections

    base = dequantize_shard(codes[0], scale_codes[0], second_scales[0])
    down_rows = lax.dynamic_slice_in_dim(down, place * own_rows, own_rows, 0)
    gain_rows = lax.dynamic_slice_in_dim(gain, place * own_rows, own_rows, 0)
    low = jnp.dot(down_rows, raised.T, preferred_element_type=F32)
    shard = ((base.astype(F32) + adapter_scale * low) * gain_rows[:, None]).astype(BF16)
    weight = lax.all_gather(shard, "fsdp", axis=0, tiled=True)

    product = jnp.dot(hidden_in, weight, preferred_element_type=F32).astype(BF16)
    mix = (
        weight[: GROUP * KVW]
        .reshape(KV_HEADS, GROUP, HEAD, KVW)
        .astype(F32)
        .sum(axis=1)
        .reshape(KVW, KVW)
        .astype(BF16)
    )
    mixes = lax.all_gather(mix, "section", axis=0)
    products = lax.all_to_all(
        product.reshape(sections, own, KVW), "section", split_axis=0, concat_axis=0, tiled=True
    )
    own_hidden = lax.dynamic_slice_in_dim(hidden_in, section * own, own, 0).astype(F32)
    own_cotangent = lax.dynamic_slice_in_dim(cotangent, section * own, own, 0).astype(F32)
    squares = jnp.sum(own_hidden * own_hidden, axis=1, keepdims=True)
    reply = pl.pallas_call(
        lambda *refs: chain_kernel(width, *refs),
        out_shape=jax.ShapeDtypeStruct((sections, own, 2 * KVW + HEAD), BF16),
        name="chain",
    )(products, mixes, collapse(own_hidden), squares, collapse(own_cotangent))
    answer = lax.all_to_all(reply, "section", split_axis=0, concat_axis=0, tiled=True)
    answer = answer.reshape(tokens, 2 * KVW + HEAD)
    direction = answer[:, :KVW]
    total = answer[:, KVW : 2 * KVW]
    slope = answer[:, 2 * KVW : 2 * KVW + 1].astype(F32)

    current = hidden_in.astype(F32) + spread(total.astype(F32), width)
    hidden_grad = lax.dot_general(
        direction, weight, (((1,), (1,)), ((), ())), preferred_element_type=F32
    )
    hidden_grad = (hidden_grad - current * slope).astype(BF16)
    pieces = lax.all_to_all(
        hidden_grad.reshape(sections, own, width),
        "section",
        split_axis=0,
        concat_axis=0,
        tiled=True,
    )
    running = own_cotangent
    sums = []
    for layer in reversed(range(sections)):
        running = running + pieces[layer].astype(F32)
        sums.append(running.astype(BF16))
    input_grad = lax.all_to_all(
        jnp.stack(sums[::-1]), "section", split_axis=0, concat_axis=0, tiled=True
    ).reshape(1, tokens, width)

    contract = (((0,), (0,)), ((), ()))
    low_grad = (
        adapter_scale * jnp.dot(direction, raised, preferred_element_type=F32)
    ).astype(BF16)
    current_bf = current.astype(BF16)
    down_grad = lax.dot_general(current_bf, low_grad, contract, preferred_element_type=F32)
    down_grad = (down_grad * gain[:, None]).astype(BF16)
    gained_down = (down.astype(F32) * gain[:, None]).astype(BF16)
    narrow = jnp.dot(current_bf, gained_down, preferred_element_type=F32).astype(BF16)
    up_grad = (
        adapter_scale
        * lax.dot_general(direction, narrow, contract, preferred_element_type=F32)
    ).astype(BF16)
    packed = jnp.concatenate(
        [down_grad.reshape(places, -1, rank), up_grad.reshape(places, -1, rank)], axis=1
    )
    arrived = lax.all_to_all(packed, "fsdp", split_axis=0, concat_axis=0, tiled=True)
    summed = arrived.astype(F32).sum(axis=0)
    return (input_grad, summed[None, :own_rows], summed[None, own_rows:])


def solution(mesh):
    return jax.shard_map(
        shards,
        mesh=mesh,
        in_specs=(
            P("section", "fsdp", None),
            P("section", "fsdp", None),
            P("section", "fsdp"),
            P("section", None),
            P("section", None, None),
            P("section", None, None),
            P("fsdp", None),
            P("fsdp", None),
        ),
        out_specs=(
            P("section", "fsdp", None),
            P("section", "fsdp", None),
            P("section", "fsdp", None),
        ),
        check_vma=False,
    )
```

time: 663 us -> 321 us (0.48)
  waiting for transfers between devices: 395 us -> 203 us
  starting transfers between devices: 104 us -> 22.2 us
  matrix products: 54 us -> 22.9 us
  local copies, waits for them, and re-layouts: 36.4 us -> 15.3 us
  other arithmetic: 40.8 us -> 24.2 us
  loops' own time: 16.3 us -> 0 us
  blocking collectives: 0 us -> 12.5 us
    ppermute x22 -> x0, waiting for transfers between devices: 272 us -> none  [from_behind(): return lax.ppermute(block, axis, route)]
    ppermute x22 -> x0, starting transfers between devices: 94.5 us -> none  [from_behind(): return lax.ppermute(block, axis, route)]
    all_gather x0 -> x1, waiting for transfers between devices: none -> 53.4 us  [shards(): mixes = lax.all_gather(mix, 'section', axis=0)]
    all_to_all x2 -> x4, waiting for transfers between devices: 33 us -> 76.2 us  [the longest x1 25.7 us: shards(): lax.all_to_all(packed, 'fsdp', split_axis=0, concat_axis=0, tiled=True)]
    dot_general x26 -> x5, matrix products: 54 us -> 22.9 us  [the longest x1 8.3 us: shards(): lax.dot_general(direction, weight, (((1,), (1,)), ((), ())), preferred_el...]
    select_n x22 -> x0, other arithmetic: 25.6 us -> none  [the longest x11 12.8 us: backward_tick(): grad_in = jnp.where(section == sections - 1, final, incoming)]
    another operation x24 -> x0, loops' own time: 16.3 us -> none  [the longest x1 7.74 us: shards(): lax.scan(forward_tick, start, jnp.arange(ticks, dtype=jnp.int32))]
    all_gather x1, waiting for transfers between devices: 90 us -> 73.6 us  [shards(): weight = lax.all_gather(shard, 'fsdp', axis=0, tiled=True)]
  transfers between devices with their start and end apart: 25 -> 6, of which waited for: 25 -> 6; matrix products, arithmetic and copies ran while one was open for 3% -> 11% of each run, Pallas kernels for 0% -> 0%
where the time goes in v1:
time: 321 us; the launch traced here: 320 us
  waiting for transfers between devices  203 us (63%)
  other arithmetic  24.2 us (8%)
  matrix products  22.9 us (7%)
  starting transfers between devices  22.2 us (7%)
  local copies, waits for them, and re-layouts  15.3 us (5%)
  between operations  14.3 us (4%)
  blocking collectives  12.5 us (4%)
  Pallas kernels  5.72 us (2%)
    all_gather x1, waiting for transfers between devices, shards(): weight = lax.all_gather(shard, 'fsdp', axis=0, tiled=True)  73.6 us
    all_gather x1, waiting for transfers between devices, shards(): mixes = lax.all_gather(mix, 'section', axis=0)  53.4 us
    all_to_all x1, waiting for transfers between devices, shards(): lax.all_to_all(packed, 'fsdp', split_axis=0, concat_axis=0, tiled=True)  25.7 us
    all_to_all x1, waiting for transfers between devices, shards(): lax.all_to_all(jnp.stack(sums[::-1]), 'section', split_axis=0, concat_axi...  25.1 us
    all_to_all x1, waiting for transfers between devices, shards(): lax.all_to_all(hidden_grad.reshape(sections, own, width), 'section', spli...  16.1 us
    unnamed x9, other arithmetic  12.7 us
    all_to_all x1, blocking collectives, shards(): lax.all_to_all(reply, 'section', split_axis=0, concat_axis=0, tiled=True)  12.5 us
    all_to_all x1, waiting for transfers between devices, shards(): lax.all_to_all(product.reshape(sections, own, KVW), 'section', split_axis...  9.18 us
  transfers between devices with their start and end apart: 6, of which 6 were waited for; matrix products, arithmetic and copies ran while one was open for 11% of the time, Pallas kernels for 0%

profile of v1, /device:TPU:32, one launch (start us, length us, event | category | flops | bytes accessed | tf_op | source)
XLA Modules:
  0.0 320.3 jit_solution(6565697755143409191)
XLA Ops:
  9.8 2.5 fusion.6
  12.4 73.6 %all-gather.3.cloned.1.call-done = bf16[8192,512]{1,0:T(8,128)(2,1)} async-done(((bf16[256,512]{1,0:T(8,128)(2,1)}), bf16[8192,512]{1,0:T(8,128)(2,1)}) %all-gather.3.cloned.1.call-update) | async-done | bytes 8388624 | tf_op jit(solution)/shard_map/all_gather | solution.py:126
  86.0 4.4 %slice.64 = bf16[4096,512]{1,0:T(8,128)(2,1)} slice(bf16[8192,512]{1,0:T(8,128)(2,1)} %all-gather.3.cloned.1.call-done), slice={[0:4096], [0:512]} | slice | bytes 8388608 | tf_op jit(solution)/shard_map/slice | solution.py:130
  90.5 3.9 %reduce = bf16[4,128,512]{2,1,0:T(8,128)(2,1)} reduce(bf16[4,8,128,512]{3,2,1,0:T(8,128)(2,1)} %bitcast.190, bf16[]{:T(256)} %constant.102), dimensions={1}, to_apply=%region_0.1.clone | reduce | flops 1835008 | bytes 4718594 | tf_op jit(solution)/shard_map/reduce_sum | solution.py:133
  96.4 5.3 %convolution_convert_fusion = bf16[512,128]{0,1:T(8,128)(2,1)} fusion(bf16[128,8192]{1,0:T(8,128)(2,1)S(1)} %copy-done.1, bf16[8192,512]{1,0:T(8,128)(2,1)} %all-gather.3.cloned.1.call-done), kind=kOutput, calls=%fused_computation.15 | convolution fusion | flops 1073807360 | bytes 10616832 | tf_op jit(solution)/shard_map/dot_general | solution.py:128
  101.7 6.5 %all-to-all-start = ((bf16[8,16,512]{2,1,0:T(8,128)(2,1)}), bf16[8,16,512]{2,1,0:T(8,128)(2,1)S(1)}, u32[]{:S(2)}, u32[]{:S(2)}) async-start(bf16[8,16,512]{2,1,0:T(8,128)(2,1)} %bitcast.9), calls=%async_computation | async-start | bytes 262144 | tf_op jit(solution)/shard_map/all_to_all | solution.py:138
  108.9 9.2 %all-to-all-done.refs_0_ = bf16[8,16,512]{2,1,0:T(8,128)(2,1)S(1)} async-done(((bf16[8,16,512]{2,1,0:T(8,128)(2,1)}), bf16[8,16,512]{2,1,0:T(8,128)(2,1)S(1)}, u32[]{:S(2)}, u32[]{:S(2)}) %all-to-all-start) | async-done | bytes 131104 | tf_op jit(solution)/shard_map/all_to_all | solution.py:138
  118.1 53.4 %all-gather.5.cloned.1.call-done.refs_1_ = bf16[8,512,512]{2,1,0:T(8,128)(2,1)} async-done(((bf16[1,512,512]{2,1,0:T(8,128)(2,1)}), bf16[8,512,512]{2,1,0:T(8,128)(2,1)}) %all-gather.5.cloned.1.call-update) | async-done | bytes 4194320 | tf_op jit(solution)/shard_map/all_gather | solution.py:137
  171.4 5.7 %chain.1 = bf16[8,16,1152]{2,1,0:T(8,128)(2,1)} custom-call(bf16[8,16,512]{2,1,0:T(8,128)(2,1)} %copy-done.4, bf16[8,512,512]{2,1,0:T(8,128)(2,1)} %all-gather.5.cloned.1.call-done.refs_1_, f32[16,512]{1,0:T(8,128)} %get-tuple-element.12.refs_2_, f32[16,1]{1,0:T(8,128)} %copy.21.refs_3_, f32[16,512]{1,0:T(8,128)} %get-tuple-element.11.refs_4_), custom_call_target="tpu_custom_call" | custom-call | tf_op jit(solution)/shard_map/chain/pallas_call | solution.py:144
  177.2 12.5 %all_to_all.25 = bf16[8,16,1152]{2,1,0:T(8,128)(2,1)S(1)} all-to-all(bf16[8,16,1152]{2,1,0:T(8,128)(2,1)} %chain.1), channel_id=1, replica_groups=mesh['section'=8,'fsdp'=32] {'section'}, dimensions={0} | all-to-all | bytes 589824 | tf_op jit(solution)/shard_map/all_to_all | solution.py:149
  191.8 8.3 %fusion = bf16[128,8192]{1,0:T(8,128)(2,1)} fusion(bf16[8192,512]{1,0:T(8,128)(2,1)} %all-gather.3.cloned.1.call-done, f32[128,4096]{1,0:T(8,128)S(1)} %bitcast.187, bf16[128,8192]{1,0:T(8,128)(2,1)S(1)} %copy-done.1, f32[128]{0:T(128)S(1)} %bitcast_convert_fusion, bf16[128,1152]{1,0:T(8,128)(2,1)S(1)} %bitcast.198), kind=kOutput, calls=%fused_computation.1 | convolution fusion | flops 1078984704 | bytes 14811648 | tf_op jit(solution)/shard_map/dot_general | solution.py:156
  200.1 4.4 %all-to-all-start.2 = ((bf16[8,16,8192]{2,1,0:T(8,128)(2,1)}), bf16[8,16,8192]{2,1,0:T(8,128)(2,1)}, u32[]{:S(2)}, u32[]{:S(2)}) async-start(bf16[8,16,8192]{2,1,0:T(8,128)(2,1)} %bitcast.193), calls=%async_computation.2 | async-start | bytes 4194304 | tf_op jit(solution)/shard_map/all_to_all | solution.py:160
  204.5 3.3 %fusion.1 = bf16[8192,64]{0,1:T(8,128)(2,1)} fusion(f32[8192]{0:T(1024)S(1)} %bitcast.206, f32[128,4096]{1,0:T(8,128)} %bitcast.188, bf16[128,8192]{1,0:T(8,128)(2,1)S(1)} %copy-done.1, bf16[128,1152]{1,0:T(8,128)(2,1)S(1)} %bitcast.199, bf16[1,512,64]{1,2,0:T(8,128)(2,1)S(1)} %copy-done), kind=kOutput, calls=%fused_computation.3 | convolution fusion | flops 146817024 | bytes 5472256 | tf_op jit(solution)/shard_map/dot_general | solution.py:181
  209.1 3.5 %fusion.7 = bf16[512,64]{0,1:T(8,128)(2,1)} fusion(bf16[1,8192,64]{1,2,0:T(8,128)(2,1)} %param.12, f32[8192]{0:T(1024)S(1)} %bitcast.207, f32[128,4096]{1,0:T(8,128)} %bitcast.189, bf16[128,8192]{1,0:T(8,128)(2,1)S(1)} %copy-done.1, bf16[128,1152]{1,0:T(8,128)(2,1)S(1)} %bitcast.200), kind=kOutput, calls=%fused_computation.17 | convolution fusion | flops 147398656 | bytes 5472256 | tf_op jit(solution)/shard_map/dot_general | solution.py:187
  215.2 16.1 %all-to-all-done.2 = bf16[8,16,8192]{2,1,0:T(8,128)(2,1)} async-done(((bf16[8,16,8192]{2,1,0:T(8,128)(2,1)}), bf16[8,16,8192]{2,1,0:T(8,128)(2,1)}, u32[]{:S(2)}, u32[]{:S(2)}) %all-to-all-start.2) | async-done | bytes 2097184 | tf_op jit(solution)/shard_map/all_to_all | solution.py:160
  231.3 7.7 %all-to-all-start.4 = ((bf16[32,272,64]{1,2,0:T(8,128)(2,1)}), bf16[32,272,64]{1,2,0:T(8,128)(2,1)S(1)}, u32[]{:S(2)}, u32[]{:S(2)}) async-start(bf16[32,272,64]{1,2,0:T(8,128)(2,1)} %pad_maximum_fusion), calls=%async_computation.4 | async-start | bytes 3145728 | tf_op jit(solution)/shard_map/all_to_all | solution.py:192
  239.0 2.6 fusion.34
  241.6 1.9 fusion.26
  243.5 1.8 bitcast_dynamic-update-slice_fusion.2
  247.8 2.0 fusion.30
  249.8 1.9 bitcast_dynamic-update-slice_fusion
  253.5 25.7 %all-to-all-done.4 = bf16[32,272,64]{1,2,0:T(8,128)(2,1)S(1)} async-done(((bf16[32,272,64]{1,2,0:T(8,128)(2,1)}), bf16[32,272,64]{1,2,0:T(8,128)(2,1)S(1)}, u32[]{:S(2)}, u32[]{:S(2)}) %all-to-all-start.4) | async-done | bytes 1114144 | tf_op jit(solution)/shard_map/all_to_all | solution.py:192
  280.4 3.6 %all-to-all-start.3 = ((bf16[8,16,8192]{2,1,0:T(8,128)(2,1)}), bf16[8,16,8192]{2,1,0:T(8,128)(2,1)S(1)}, u32[]{:S(2)}, u32[]{:S(2)}) async-start(bf16[8,16,8192]{2,1,0:T(8,128)(2,1)} %fusion.32), calls=%async_computation.3 | async-start | bytes 4194304 | tf_op jit(solution)/shard_map/all_to_all | solution.py:172
  287.0 25.1 %all-to-all-done.3 = bf16[8,16,8192]{2,1,0:T(8,128)(2,1)S(1)} async-done(((bf16[8,16,8192]{2,1,0:T(8,128)(2,1)}), bf16[8,16,8192]{2,1,0:T(8,128)(2,1)S(1)}, u32[]{:S(2)}, u32[]{:S(2)}) %all-to-all-start.3) | async-done | bytes 2097184 | tf_op jit(solution)/shard_map/all_to_all | solution.py:172
  (51 shorter events, 21.0 us)
Async XLA Ops:
  7.2 2.6 copy-start
  7.2 78.8 %all-gather.3.cloned.1.call-start = ((), (), s32[]{:S(2)}) async-start(), calls=%async_computation.5 | async-start | bytes 8650752 | tf_op jit(solution)/shard_map/all_gather | solution.py:126
  12.3 159.1 %all-gather.5.cloned.1.call-start = ((), (), s32[]{:S(2)}) async-start(), calls=%async_computation.6 | async-start | bytes 4718592 | tf_op jit(solution)/shard_map/all_gather | solution.py:137
  90.5 3.9 %copy-start.1 = (bf16[128,8192]{1,0:T(8,128)(2,1)S(1)}, bf16[128,8192]{1,0:T(8,128)(2,1)}, u32[]{:S(2)}) copy-start(bf16[128,8192]{1,0:T(8,128)(2,1)} %param.14) | copy-start | bytes 6291460
  101.7 16.3 %all-to-all-start = ((bf16[8,16,512]{2,1,0:T(8,128)(2,1)}), bf16[8,16,512]{2,1,0:T(8,128)(2,1)S(1)}, u32[]{:S(2)}, u32[]{:S(2)}) async-start(bf16[8,16,512]{2,1,0:T(8,128)(2,1)} %bitcast.9), calls=%async_computation | async-start | bytes 262144 | tf_op jit(solution)/shard_map/all_to_all | solution.py:138
  118.1 53.4 %copy-start.4 = (bf16[8,16,512]{2,1,0:T(8,128)(2,1)}, bf16[8,16,512]{2,1,0:T(8,128)(2,1)S(1)}, u32[]{:S(2)}) copy-start(bf16[8,16,512]{2,1,0:T(8,128)(2,1)S(1)} %all-to-all-done.refs_0_) | copy-start | bytes 393220
  191.8 8.3 %copy-start.2 = (f32[16,8,32,128]{3,1,2,0:T(8,128)}, f32[16,8,32,128]{3,1,2,0:T(8,128)S(1)}, u32[]{:S(2)}) copy-start(f32[16,8,32,128]{3,1,2,0:T(8,128)S(1)} %copy.40) | copy-start | bytes 6291460
  200.1 31.2 %all-to-all-start.2 = ((bf16[8,16,8192]{2,1,0:T(8,128)(2,1)}), bf16[8,16,8192]{2,1,0:T(8,128)(2,1)}, u32[]{:S(2)}, u32[]{:S(2)}) async-start(bf16[8,16,8192]{2,1,0:T(8,128)(2,1)} %bitcast.193), calls=%async_computation.2 | async-start | bytes 4194304 | tf_op jit(solution)/shard_map/all_to_all | solution.py:160
  231.3 47.9 %all-to-all-start.4 = ((bf16[32,272,64]{1,2,0:T(8,128)(2,1)}), bf16[32,272,64]{1,2,0:T(8,128)(2,1)S(1)}, u32[]{:S(2)}, u32[]{:S(2)}) async-start(bf16[32,272,64]{1,2,0:T(8,128)(2,1)} %pad_maximum_fusion), calls=%async_computation.4 | async-start | bytes 3145728 | tf_op jit(solution)/shard_map/all_to_all | solution.py:192
  279.2 1.2 copy-start.3
  280.4 31.7 %all-to-all-start.3 = ((bf16[8,16,8192]{2,1,0:T(8,128)(2,1)}), bf16[8,16,8192]{2,1,0:T(8,128)(2,1)S(1)}, u32[]{:S(2)}, u32[]{:S(2)}) async-start(bf16[8,16,8192]{2,1,0:T(8,128)(2,1)} %fusion.32), calls=%async_computation.3 | async-start | bytes 4194304 | tf_op jit(solution)/shard_map/all_to_all | solution.py:172
Sparse Core Ops, SparseCore 0:
  12.5 73.5 all-gather.2
  94.5 76.8 all-gather.4

commit v2 on v1

v2 whole, which is shorter than its diff:
```python
import functools

import jax
import jax.numpy as jnp
from jax import lax
from jax.experimental import pallas as pl
from jax.experimental.pallas import tpu as pltpu
from jax.sharding import PartitionSpec as P

HEAD = 128
GROUP = 8
KV_HEADS = 4
KVW = KV_HEADS * HEAD
BLOCK = 64
SROWS = 32

NF4_TABLE = (
    -1.0,
    -0.6961928009986877,
    -0.5250730514526367,
    -0.39491748809814453,
    -0.28444138169288635,
    -0.18477343022823334,
    -0.09105003625154495,
    0.0,
    0.07958029955625534,
    0.16093020141124725,
    0.24611230194568634,
    0.33791524171066284,
    0.44070982933044434,
    0.5626170039176941,
    0.7229568362236023,
    1.0,
)
adapter_scale = 0.5
epsilon = 1e-05
F32 = jnp.float32
BF16 = jnp.bfloat16


def dequantize_shard(codes, scale_codes, second_scales):
    value_rows = jnp.zeros(codes.shape, jnp.float32)
    for entry in range(16):
        value_rows = jnp.where(codes == entry, jnp.float32(NF4_TABLE[entry]), value_rows)
    outer = jnp.repeat(second_scales, SROWS)
    block = outer[:, None] * (scale_codes.astype(jnp.float32) + 1.0) / 256.0
    scaled = value_rows.reshape(codes.shape[0], scale_codes.shape[1], BLOCK) * block[:, :, None]
    return scaled.reshape(codes.shape).astype(jnp.bfloat16)


def chip_kernel(
    width,
    shard,
    hidden_hbm,
    cotangent_hbm,
    gained_hbm,
    raised,
    out,
    grad_out,
    weight,
    mixes,
    hidden,
    cotangent,
    gained,
    product,
    product_send,
    product_recv,
    folded,
    descent,
    squares,
    totals,
    values,
    inverses,
    scaled_send,
    total_send,
    slope_send,
    scaled,
    total,
    slopes,
    pair_send,
    odd,
    pair_recv,
    later_send,
    later,
    other_send,
    grad_send,
    grad_recv,
    narrow,
    local_sem,
    send_sem,
    weight_sem,
    mix_sem,
    product_sem,
    reply_sem,
    pair_sem,
    later_sem,
    other_sem,
    grad_send_sem,
    grad_sem,
):
    section = lax.axis_index("section")
    place = lax.axis_index("fsdp")
    y, xh = section // 2, section % 2
    xl, z, core = place // 16, (place // 2) % 8, place % 2
    half_width = width // 2
    column_base = xh * half_width
    layers = 2 * 4

    def device(to_section, to_place):
        return (to_section, to_place)

    mate = device(section, 2 * (place // 2) + 1 - core)
    across = device(section, (place + 16) % 32)
    above = device(section, xl * 16 + ((z + 1) % 8) * 2 + core)
    below = device(section, xl * 16 + ((z + 7) % 8) * 2 + core)
    twin = 2 * y + 1 - xh
    swap = device(twin, (place + 16) % 32)
    used = [0]

    def transfer(source, target, arrival, to, sem=None):
        if sem is None:
            sem = send_sem.at[used[0]]
            used[0] += 1
        copy = pltpu.make_async_remote_copy(
            src_ref=source,
            dst_ref=target,
            send_sem=sem,
            recv_sem=arrival,
            device_id=to,
            device_id_type=pl.DeviceIdType.MESH,
        )
        copy.start()
        return copy

    def arrive(target, arrival):
        pltpu.make_async_remote_copy(
            src_ref=target,
            dst_ref=target,
            send_sem=send_sem.at[0],
            recv_sem=arrival,
            device_id=mate,
            device_id_type=pl.DeviceIdType.MESH,
        ).wait_recv()

    loads = [
        pltpu.make_async_copy(hidden_hbm, hidden, local_sem.at[0]),
        pltpu.make_async_copy(cotangent_hbm, cotangent, local_sem.at[1]),
        pltpu.make_async_copy(gained_hbm, gained, local_sem.at[2]),
    ]
    for load in loads:
        load.start()

    barrier = pltpu.get_barrier_semaphore()

    def greet(to):
        pl.semaphore_signal(
            barrier, inc=1, device_id=to, device_id_type=pl.DeviceIdType.MESH
        )

    def greet_place(step, carry):
        greet(device(section, (place + step) % 32))
        return carry

    lax.fori_loop(1, 32, greet_place, 0)
    for step in range(1, layers):
        greet(device((section + step) % 8, place))
    greet(swap)
    pl.semaphore_wait(barrier, 31 + 7 + 1)

    pending = []

    def slot(x, depth, which):
        return x * 16 + depth * 2 + which

    def half(block, h):
        return weight.at[block, pl.ds(h * 128, 128)]

    def pass_on(block, h, to):
        pending.append(transfer(half(block, h), half(block, h), weight_sem.at[block * 2 + h], to))

    def await_block(block, h):
        arrive(half(block, h), weight_sem.at[block * 2 + h])

    swapped_place = (place + 16) % 32

    @pl.when(xl != xh)
    def _():
        for h in range(2):
            transfer(
                shard.at[pl.ds(h * 128, 128)],
                half(swapped_place, h),
                weight_sem.at[swapped_place * 2 + h],
                swap,
                local_sem.at[3 + h],
            )

    @pl.when(xl == xh)
    def _():
        pltpu.make_async_copy(shard, weight.at[place], local_sem.at[3]).start()

    loads[0].wait()
    loads[1].wait()
    loads[2].wait()
    rows = pl.ds(y * 32, 32)

    def fold(ref):
        for head in range(KV_HEADS):
            part = jnp.zeros((32, HEAD), F32)
            for member in range(GROUP):
                at = (head * GROUP + member) * HEAD
                part += ref[rows, pl.ds(at, HEAD)].astype(F32)
            yield head, part

    @pl.when(xl == xh)
    def _():
        pltpu.make_async_copy(shard, weight.at[place], local_sem.at[3]).wait()

    others = [place, slot(1 - xl, z, core)]
    for h in range(2):

        @pl.when(xl != xh)
        def _():
            await_block(place, h)

        if h == 0:
            pass_on(place, h, across)
        for to in (above, below, mate):
            pass_on(place, h, to)
    for head, part in fold(hidden):
        folded[:, head * HEAD : (head + 1) * HEAD] = part
    for head, part in fold(cotangent):
        descent[:, head * HEAD : (head + 1) * HEAD] = part
    square = jnp.zeros((32, HEAD), F32)
    for at in range(0, width, HEAD):
        piece = hidden[rows, pl.ds(at, HEAD)].astype(F32)
        square += piece * piece
    squares[...] = jnp.broadcast_to(jnp.sum(square, axis=1, keepdims=True), (32, HEAD))
    product[...] = jnp.zeros_like(product)

    await_block(others[1], 0)
    for to in (above, below, mate):
        pass_on(others[1], 0, to)

    def at_distance(distance):
        if distance == 0:
            return [z]
        if distance == 4:
            return [(z + 4) % 8]
        return [(z + 8 - distance) % 8, (z + distance) % 8]

    def multiply(distance, which):
        depths = len(at_distance(distance))

        def step(index, carry):
            x = index // depths
            depth = (z + 8 - distance + (index % depths) * 2 * distance) % 8
            block = slot(x, depth, which)
            columns = pl.ds(pl.multiple_of(column_base + (depth * 2 + which) * 256, 256), 256)
            product[x] += jnp.dot(hidden[:, columns], weight[block], preferred_element_type=F32)
            return carry

        lax.fori_loop(0, 2 * depths, step, 0)

    def relay_across(distance):
        for depth in at_distance(distance):
            block = slot(1 - xl, depth, core)
            await_block(block, 1)
            pass_on(block, 1, mate)

    def await_mate(distance):
        for depth in at_distance(distance):
            for x in range(2):
                for h in range(2):
                    await_block(slot(x, depth, 1 - core), h)

    for distance in range(1, 5):
        low, high = (z + 8 - distance) % 8, (z + distance) % 8
        for x, h, up_reach, down_reach in ((xl, 0, 4, 3), (1 - xl, 0, 3, 4), (xl, 1, 4, 3)):
            for depth, reach, onward in ((low, up_reach, above), (high, down_reach, below)):
                if distance > reach:
                    continue
                block = slot(x, depth, core)
                await_block(block, h)
                if distance < reach:
                    pass_on(block, h, onward)
                pass_on(block, h, mate)
                if h == 1:
                    pass_on(block, h, across)
        if distance == 1:
            pass_on(place, 1, across)
        relay_across(distance - 1)
        multiply(distance - 1, core)
        if distance >= 2:
            await_mate(distance - 2)
            multiply(distance - 2, 1 - core)
    relay_across(4)
    multiply(4, core)
    for distance in (3, 4):
        await_mate(distance)
        multiply(distance, 1 - core)

    @pl.when(xh == 0)
    def _():
        for pair in range(2):
            for head in range(KV_HEADS):

                def add(index, carry):
                    block = pair * 16 + head * 4 + index
                    return (
                        carry
                        + weight[block, :128].astype(F32)
                        + weight[block, 128:].astype(F32)
                    )

                mix = lax.fori_loop(0, 4, add, jnp.zeros((HEAD, KVW), F32))
                mixes[2 * y + pair, head * HEAD : (head + 1) * HEAD] = mix.astype(BF16)

    product_send[...] = product[...].astype(BF16)
    y_up, y_down = (y + 1) % 4, (y + 3) % 4
    y_far = (y + 2) % 4
    mix_base = used[0]
    used[0] += 8

    def mix_block(which_y, which, part=None):
        if part is None:
            return mixes.at[pl.ds(2 * which_y, 2), pl.ds(which * 256, 256)]
        return mixes.at[pl.ds(2 * which_y, 2), pl.ds(which * 256 + part * 128, 128)]

    mix_moves = (
        (mix_block(y, core), 0, (2 * y_up, place)),
        (mix_block(y, core), 1, (2 * y_down, place)),
        (mix_block(y_down, core, 0), 2, (2 * y_up, place)),
        (mix_block(y_up, core, 1), 3, (2 * y_down, place)),
        (mix_block(y_down, core), 4, mate),
        (mix_block(y_up, core), 5, mate),
        (mix_block(y_far, core, 0), 6, mate),
        (mix_block(y_far, core, 1), 7, mate),
    )

    def start_mix(index):
        block, sem, to = mix_moves[index]
        return transfer(block, block, mix_sem.at[sem], to, send_sem.at[mix_base + index])

    @pl.when(xh == 0)
    def _():
        start_mix(0)
        start_mix(1)

    product_base = used[0]
    used[0] += 4

    def send_product(step):
        to_y = (y + step) % 4
        return transfer(
            product_send.at[:, pl.ds(to_y * 32, 32)],
            product_recv.at[section],
            product_sem.at[section],
            (2 * to_y, place),
            send_sem.at[product_base + step],
        )

    for step in range(1, 4):
        pending.append(send_product(step))

    @pl.when(xh == 1)
    def _():
        send_product(0)

    reply_base = used[0]
    used[0] += 24

    def reply_copies(step, to_column):
        to_y = (y + step) % 4
        to = (2 * to_y + to_column, place)
        at = reply_base + (step * 2 + to_column) * 3
        yield (
            scaled_send.at[pl.ds(2 * to_y, 2)],
            scaled.at[:, pl.ds(y * 32, 32)],
            reply_sem.at[y * 3],
            to,
            send_sem.at[at],
        )
        yield (
            slope_send.at[to_y],
            slopes.at[pl.ds(y * 32, 32)],
            reply_sem.at[y * 3 + 1],
            to,
            send_sem.at[at + 1],
        )
        if to_column == 0:
            yield (
                total_send.at[pl.ds(2 * to_y, 2)],
                total.at[:, pl.ds(y * 32, 32)],
                reply_sem.at[y * 3 + 2],
                to,
                send_sem.at[at + 2],
            )
        else:
            yield (
                total_send.at[2 * to_y + 1],
                total.at[1, pl.ds(y * 32, 32)],
                reply_sem.at[y * 3 + 2],
                to,
                send_sem.at[at + 2],
            )

    @pl.when(xh == 0)
    def _():
        product_recv[section] = product_send[:, rows]
        arrive(mix_block(y_down, core), mix_sem.at[0])
        start_mix(2)
        start_mix(4)
        arrive(mix_block(y_up, core), mix_sem.at[1])
        start_mix(3)
        start_mix(5)
        arrive(mix_block(y_far, core, 0), mix_sem.at[2])
        start_mix(6)
        arrive(mix_block(y_far, core, 1), mix_sem.at[3])
        start_mix(7)
        arrive(product_recv.at[section + 1], product_sem.at[section + 1])
        for step in range(1, 4):
            for column in range(2):
                sender = 2 * ((y + step) % 4) + column
                arrive(product_recv.at[sender], product_sem.at[sender])
        arrive(mix_block(y_down, 1 - core), mix_sem.at[4])
        arrive(mix_block(y_up, 1 - core), mix_sem.at[5])
        arrive(mix_block(y_far, 1 - core, 0), mix_sem.at[6])
        arrive(mix_block(y_far, 1 - core, 1), mix_sem.at[7])

        square_sum = squares[:, :1]
        running = jnp.zeros((32, KVW), F32)
        for layer in range(layers):
            moved = 2.0 * folded[...] + GROUP * running
            energy = square_sum + jnp.sum(running * moved, axis=1, keepdims=True)
            inverse = 1.0 / jnp.sqrt(energy / width + epsilon)
            pair_at = layer - layer % 2
            mixed = product_recv[pair_at, layer % 2].astype(F32) + product_recv[
                pair_at + 1, layer % 2
            ].astype(F32)
            if layer:
                mixed += jnp.dot(running.astype(BF16), mixes[layer], preferred_element_type=F32)
            value = mixed * inverse
            totals[layer] = running
            values[layer] = value
            inverses[layer] = jnp.broadcast_to(inverse, (32, HEAD))
            total_send[layer] = running.astype(BF16)
            running = running + value
        direction = descent[...]
        for layer in reversed(range(layers)):
            inverse = inverses[layer][:, :1]
            slope = (
                jnp.sum(direction * values[layer], axis=1, keepdims=True)
                / width
                * inverse
                * inverse
            )
            step_scaled = (direction * inverse).astype(BF16)
            scaled_send[layer] = step_scaled
            at = (layer % 2) * 64
            slope_send[layer // 2, :, at : at + 64] = jnp.broadcast_to(slope, (32, 64))
            if layer:
                direction = (
                    direction
                    + lax.dot_general(
                        step_scaled,
                        mixes[layer],
                        (((1,), (1,)), ((), ())),
                        preferred_element_type=F32,
                    )
                    - (folded[...] + GROUP * totals[layer]) * slope
                )
        for item in range(3):
            for step in (1, 2, 3, 0):
                for column in range(2):
                    if step == 0 and column == 0:
                        continue
                    transfer(*list(reply_copies(step, column))[item])
        scaled[:, rows] = scaled_send[pl.ds(2 * y, 2)]
        total[:, rows] = total_send[pl.ds(2 * y, 2)]
        slopes[rows] = slope_send[y]

    def await_reply(step):
        from_y = (y + step) % 4
        token_rows = pl.ds(from_y * 32, 32)
        arrive(scaled.at[:, token_rows], reply_sem.at[from_y * 3])
        arrive(slopes.at[token_rows], reply_sem.at[from_y * 3 + 1])

        @pl.when(xh == 0)
        def _():
            arrive(total.at[:, token_rows], reply_sem.at[from_y * 3 + 2])

        @pl.when(xh == 1)
        def _():
            arrive(total.at[1, token_rows], reply_sem.at[from_y * 3 + 2])

    for step in range(1, 4):
        await_reply(step)

    @pl.when(xh == 1)
    def _():
        await_reply(0)

    column_flag = (1 - xh).astype(F32)
    pair_base = used[0]
    used[0] += 28
    quarter = half_width // 4

    def pair_copy(q, step):
        to_y = (y + step) % 4
        columns = pl.ds(q * quarter, quarter)
        return (
            pair_send.at[pl.ds(to_y * 32, 32), columns],
            pair_recv.at[y, :, columns],
            pair_sem.at[y * 4 + q],
            (2 * to_y + xh, place),
            send_sem.at[pair_base + q * 3 + step - 1],
        )

    def later_copy(q, step):
        to_y = (y + step) % 4
        columns = pl.ds(q * quarter, quarter)
        return (
            later_send.at[to_y, :, columns],
            later.at[pl.ds(y * 32, 32), columns],
            later_sem.at[y * 4 + q],
            (2 * to_y + xh, place),
            send_sem.at[pair_base + 12 + q * 3 + step - 1],
        )

    def other_copy(q):
        return (
            other_send.at[:, pl.ds(q * quarter, quarter)],
            out.at[:, pl.ds(pl.multiple_of(column_base + q * quarter, quarter), quarter)],
            other_sem.at[q],
            (twin, place),
            send_sem.at[pair_base + 24 + q],
        )

    def hidden_gradients(q):
        def step(index, carry):
            block = q * 4 + index
            at = pl.multiple_of(block * 256, 256)
            columns = pl.ds(pl.multiple_of(column_base + at, 256), 256)
            part = hidden[:, columns].astype(F32)
            grads = []
            for pair in range(2):
                shift = jnp.where(
                    xh == 0, total[pair, :, q * HEAD : (q + 1) * HEAD].astype(F32), 0.0
                )
                current = part + jnp.concatenate([shift, shift], axis=1)
                slope = slopes[:, pair * 64 : pair * 64 + 1]
                grads.append(
                    lax.dot_general(
                        scaled[pair],
                        weight[pair * 16 + block],
                        (((1,), (1,)), ((), ())),
                        preferred_element_type=F32,
                    )
                    - current * slope
                )
            odd[:, pl.ds(at, 256)] = grads[1].astype(BF16)
            pair_send[:, pl.ds(at, 256)] = (grads[0] + grads[1]).astype(BF16)
            return carry

        lax.fori_loop(0, 4, step, 0)

        @pl.when(y >= 1)
        def _():
            for step in range(1, 4):
                transfer(*pair_copy(q, step))

    def suffix(q):
        columns = pl.ds(q * quarter, quarter)
        for step in range(1, 4):
            from_y = (y + step) % 4

            @pl.when(from_y >= 1)
            def _():
                arrive(pair_recv.at[from_y, :, columns], pair_sem.at[from_y * 4 + q])

        @pl.when(y >= 1)
        def _():
            pair_recv[y, :, columns] = pair_send[rows, columns]

        running = pair_recv[3, :, columns].astype(F32)
        later_send[2, :, columns] = running.astype(BF16)
        running += pair_recv[2, :, columns].astype(F32)
        later_send[1, :, columns] = running.astype(BF16)
        running += pair_recv[1, :, columns].astype(F32)
        later_send[0, :, columns] = running.astype(BF16)
        for step in range(1, 4):
            to_y = (y + step) % 4

            @pl.when(to_y < 3)
            def _():
                transfer(*later_copy(q, step))

        @pl.when(y < 3)
        def _():
            later[rows, columns] = later_send[y, :, columns]

        @pl.when(y == 3)
        def _():
            later[:, columns] = jnp.zeros((128, quarter), BF16)

    def finish(q):
        @pl.when(y < 3)
        def _():
            for step in range(1, 4):
                from_y = (y + step) % 4
                target = later.at[pl.ds(from_y * 32, 32), pl.ds(q * quarter, quarter)]
                arrive(target, later_sem.at[from_y * 4 + q])

        def step(index, carry):
            at = pl.multiple_of(q * quarter + index * 256, 256)
            columns = pl.ds(at, 256)
            own_columns = pl.ds(pl.multiple_of(column_base + at, 256), 256)
            start = cotangent[:, own_columns].astype(F32) + later[:, columns].astype(F32)
            even_grad = (start + pair_send[:, columns].astype(F32)).astype(BF16)
            odd_grad = (start + odd[:, columns].astype(F32)).astype(BF16)
            out[:, own_columns] = jnp.where(xh == 0, even_grad, odd_grad)
            other_send[:, columns] = jnp.where(xh == 0, odd_grad, even_grad)
            return carry

        lax.fori_loop(0, 4, step, 0)
        pending.append(transfer(*other_copy(q)))

    def adapter_setup():
        low = lax.dot_general(
            raised[...], scaled[xh], (((0,), (1,)), ((), ())), preferred_element_type=F32
        )
        return (adapter_scale * low).astype(BF16)

    def current_columns(block):
        columns = pl.ds(pl.multiple_of(block * 256, 256), 256)
        part = hidden[:, columns].astype(F32)
        head = jnp.minimum(block // 4, KV_HEADS - 1)
        shift = total[xh, :, pl.ds(pl.multiple_of(head * HEAD, HEAD), HEAD)].astype(F32)
        shift = jnp.where(block < 16, shift, 0.0)
        return (part + jnp.concatenate([shift, shift], axis=1)).astype(BF16)

    low = adapter_setup_holder = None

    def adapter_narrow(block, carry):
        current = current_columns(block)
        rows_at = pl.ds(pl.multiple_of(block * 256, 256), 256)
        return carry + jnp.dot(current, gained[rows_at], preferred_element_type=F32)

    def adapter_up():
        total_narrow = lax.fori_loop(0, 32, adapter_narrow, jnp.zeros((128, 64), F32))
        narrow[...] = total_narrow.astype(BF16)
        up_grad = adapter_scale * lax.dot_general(
            scaled[xh], narrow[...], (((0,), (0,)), ((), ())), preferred_element_type=F32
        )
        padded = jnp.concatenate([up_grad, jnp.zeros((KVW, 192), F32)], axis=1)
        grad_send[:, 64:] = padded.astype(BF16).reshape(32, 16, 256)

    def adapter_down(low):
        def step(block, carry):
            grad = jnp.dot(low, current_columns(block), preferred_element_type=F32)
            grad_send[block, :64] = grad.astype(BF16)
            return carry

        lax.fori_loop(0, 32, step, 0)

    def grad_copy(step):
        to = (place + step) % 32
        return (
            grad_send.at[to],
            grad_recv.at[place],
            grad_sem.at[place],
            device(section, to),
            grad_send_sem.at[step],
        )

    def send_grads(step, carry):
        transfer(*grad_copy(step))
        return carry

    for q in range(4):
        hidden_gradients(q)
    suffix(0)
    suffix(1)
    adapter_up()
    suffix(2)
    finish(0)
    suffix(3)
    finish(1)
    adapter_down(adapter_setup())
    lax.fori_loop(1, 32, send_grads, 0)
    finish(2)
    finish(3)
    grad_recv[place] = grad_send[place]

    def await_grads(step, carry):
        sender = (place + 32 - step) % 32
        arrive(grad_recv.at[sender], grad_sem.at[sender])
        return carry

    lax.fori_loop(1, 32, await_grads, 0)

    def sum_grads(index, carry):
        return carry + grad_recv[index].astype(F32)

    grad_out[...] = lax.fori_loop(0, 32, sum_grads, jnp.zeros((80, 256), F32))
    for q in range(4):
        columns = pl.ds(
            pl.multiple_of((1 - xh) * half_width + q * quarter, quarter), quarter
        )
        arrive(out.at[:, columns], other_sem.at[q])

    def gone(copy):
        source, target, arrival, to, sem = copy
        pltpu.make_async_remote_copy(
            src_ref=source,
            dst_ref=target,
            send_sem=sem,
            recv_sem=arrival,
            device_id=to,
            device_id_type=pl.DeviceIdType.MESH,
        ).wait_send()

    for copy in pending:
        copy.wait_send()

    @pl.when(xl != xh)
    def _():
        for h in range(2):
            gone(
                (
                    shard.at[pl.ds(h * 128, 128)],
                    half(swapped_place, h),
                    weight_sem.at[swapped_place * 2 + h],
                    swap,
                    local_sem.at[3 + h],
                )
            )

    @pl.when(xh == 0)
    def _():
        for index in range(8):
            block, sem, to = mix_moves[index]
            gone((block, block, mix_sem.at[sem], to, send_sem.at[mix_base + index]))
        for step in range(4):
            for column in range(2):
                if step or column:
                    for copy in reply_copies(step, column):
                        gone(copy)

    @pl.when(xh == 1)
    def _():
        gone(
            (
                product_send.at[:, pl.ds(y * 32, 32)],
                product_recv.at[section],
                product_sem.at[section],
                (2 * y, place),
                send_sem.at[product_base],
            )
        )

    @pl.when(y >= 1)
    def _():
        for q in range(4):
            for step in range(1, 4):
                gone(pair_copy(q, step))

    for step in range(1, 4):

        @pl.when((y + step) % 4 < 3)
        def _():
            for q in range(4):
                gone(later_copy(q, step))

    def grads_gone(step, carry):
        gone(grad_copy(step))
        return carry

    lax.fori_loop(1, 32, grads_gone, 0)
    assert used[0] <= SENDS, used


SENDS = 256


def shards(
    codes,
    scale_codes,
    second_scales,
    gains,
    down_adapter,
    up_projection_weight,
    hidden_in,
    cotangent,
):
    place = lax.axis_index("fsdp")
    gain = gains[0].astype(F32)
    down = down_adapter[0]
    raised = up_projection_weight[0]
    tokens, width = hidden_in.shape
    own_rows = codes.shape[1]

    base = dequantize_shard(codes[0], scale_codes[0], second_scales[0])
    down_rows = lax.dynamic_slice_in_dim(down, place * own_rows, own_rows, 0)
    gain_rows = lax.dynamic_slice_in_dim(gain, place * own_rows, own_rows, 0)
    low = jnp.dot(down_rows, raised.T, preferred_element_type=F32)
    shard = ((base.astype(F32) + adapter_scale * low) * gain_rows[:, None]).astype(BF16)
    gained = (down.astype(F32) * gain[:, None]).astype(BF16)
    vmem = pl.BlockSpec(memory_space=pltpu.VMEM)
    hbm = pl.BlockSpec(memory_space=pl.ANY)
    dma = pltpu.SemaphoreType.DMA
    input_grad, grads = pl.pallas_call(
        functools.partial(chip_kernel, width),
        out_shape=(
            jax.ShapeDtypeStruct((tokens, width), BF16),
            jax.ShapeDtypeStruct((80, 256), F32),
        ),
        in_specs=[vmem, hbm, hbm, hbm, vmem],
        out_specs=(vmem, vmem),
        scratch_shapes=[
            pltpu.VMEM((32, 256, KVW), BF16),
            pltpu.VMEM((8, KVW, KVW), BF16),
            pltpu.VMEM((tokens, width), BF16),
            pltpu.VMEM((tokens, width), BF16),
            pltpu.VMEM((width, 64), BF16),
            pltpu.VMEM((2, tokens, KVW), F32),
            pltpu.VMEM((2, tokens, KVW), BF16),
            pltpu.VMEM((8, 2, 32, KVW), BF16),
            pltpu.VMEM((32, KVW), F32),
            pltpu.VMEM((32, KVW), F32),
            pltpu.VMEM((32, HEAD), F32),
            pltpu.VMEM((8, 32, KVW), F32),
            pltpu.VMEM((8, 32, KVW), F32),
            pltpu.VMEM((8, 32, HEAD), F32),
            pltpu.VMEM((8, 32, KVW), BF16),
            pltpu.VMEM((8, 32, KVW), BF16),
            pltpu.VMEM((4, 32, HEAD), F32),
            pltpu.VMEM((2, tokens, KVW), BF16),
            pltpu.VMEM((2, tokens, KVW), BF16),
            pltpu.VMEM((tokens, HEAD), F32),
            pltpu.VMEM((tokens, width // 2), BF16),
            pltpu.VMEM((tokens, width // 2), BF16),
            pltpu.VMEM((4, 32, width // 2), BF16),
            pltpu.VMEM((3, 32, width // 2), BF16),
            pltpu.VMEM((tokens, width // 2), BF16),
            pltpu.VMEM((tokens, width // 2), BF16),
            pltpu.VMEM((32, 80, 256), BF16),
            pltpu.VMEM((32, 80, 256), BF16),
            pltpu.VMEM((tokens, 64), BF16),
            dma((5,)),
            dma((SENDS,)),
            dma((64,)),
            dma((8,)),
            dma((8,)),
            dma((12,)),
            dma((16,)),
            dma((16,)),
            dma((4,)),
            dma((32,)),
            dma((32,)),
        ],
        compiler_params=pltpu.CompilerParams(
            collective_id=0, has_side_effects=True, vmem_limit_bytes=58 * 2**20
        ),
        name="relay",
    )(shard, hidden_in, cotangent, gained, raised)
    down_grad = grads[:64].T * gain_rows[:, None]
    return (input_grad[None], down_grad[None], grads[None, 64:, :64])


def solution(mesh):
    return jax.shard_map(
        shards,
        mesh=mesh,
        in_specs=(
            P("section", "fsdp", None),
            P("section", "fsdp", None),
            P("section", "fsdp"),
            P("section", None),
            P("section", None, None),
            P("section", None, None),
            P("fsdp", None),
            P("fsdp", None),
        ),
        out_specs=(
            P("section", "fsdp", None),
            P("section", "fsdp", None),
            P("section", "fsdp", None),
        ),
        check_vma=False,
    )
```

time: 321 us -> 183 us (0.57)
  waiting for transfers between devices: 203 us -> 0 us
  Pallas kernels: 5.72 us -> 166 us
  starting transfers between devices: 22.2 us -> 0 us
  matrix products: 22.9 us -> 2.65 us
  other arithmetic: 24.2 us -> 5.18 us
  between operations: 14.3 us -> 0.69 us
  blocking collectives: 12.5 us -> 0 us
  local copies, waits for them, and re-layouts: 15.3 us -> 8.1 us
    pallas_call x1, Pallas kernels: 5.72 us -> 166 us  [shards(): pl.pallas_call(functools.partial(chip_kernel, width), out_shape=(jax.Shap...]
    all_gather x2 -> x0, waiting for transfers between devices: 127 us -> none  [the longest x1 73.6 us: shards(): weight = lax.all_gather(shard, 'fsdp', axis=0, tiled=True)]
    all_to_all x4 -> x0, waiting for transfers between devices: 76.2 us -> none  [the longest x1 25.7 us: shards(): lax.all_to_all(packed, 'fsdp', split_axis=0, concat_axis=0, tiled=True)]
    all_to_all x4 -> x0, starting transfers between devices: 22.1 us -> none  [the longest x1 7.67 us: shards(): lax.all_to_all(packed, 'fsdp', split_axis=0, concat_axis=0, tiled=True)]
    dot_general x4 -> x0, matrix products: 20.4 us -> none  [the longest x1 8.3 us: shards(): lax.dot_general(direction, weight, (((1,), (1,)), ((), ())), preferred_el...]
    unnamed x9 -> x0, other arithmetic: 12.7 us -> none
    all_to_all x1 -> x0, blocking collectives: 12.5 us -> none  [shards(): lax.all_to_all(reply, 'section', split_axis=0, concat_axis=0, tiled=True)]
    reduce_sum x3 -> x0, other arithmetic: 5.75 us -> none  [the longest x1 3.89 us: shards(): mix = weight[:GROUP * KVW].reshape(KV_HEADS, GROUP, HEAD, KVW).astype(F32...]
  transfers between devices with their start and end apart: 6 -> 0, of which waited for: 6 -> 0; matrix products, arithmetic and copies ran while one was open for 11% -> 0% of each run, Pallas kernels for 0% -> 0%
where the time goes in v2:
time: 183 us
  Pallas kernels  166 us (91%)
  local copies, waits for them, and re-layouts  8.1 us (4%)
  other arithmetic  5.18 us (3%)
  matrix products  2.65 us (1%)
    pallas_call x1, Pallas kernels, shards(): pl.pallas_call(functools.partial(chip_kernel, width), out_shape=(jax.Shap...  166 us
    unnamed x5, local copies, waits for them, and re-layouts  5.76 us

profile of v2, /device:TPU:32, one launch (start us, length us, event | category | flops | bytes accessed | tf_op | source)
XLA Modules:
  0.0 183.0 jit_solution(16270098945348869604)
XLA Ops:
  0.6 0.7 broadcast_in_dim.85
  1.4 0.1 mul.62
  1.4 0.7 fusion.9
  2.1 0.8 convert_element_type.39
  3.0 1.6 copy.15
  4.6 0.2 copy.14
  4.8 0.0 copy-start
  4.8 2.6 %fusion.3.shard = bf16[256,512]{1,0:T(8,128)(2,1)} fusion(f32[256]{0:T(256)S(1)} %bitcast.41, f32[256,512]{1,0:T(8,128)S(1)} %copy.14, s32[1,256,512]{2,1,0:T(8,128)} %param.8, bf16[1,512,64]{1,2,0:T(8,128)(2,1)} %param.13, bf16[1,8192,64]{1,2,0:T(8,128)(2,1)} %param.12, s32[]{:T(128)S(6)} %select_n.107), kind=kOutput, calls=%fused_computation.5 | convolution fusion | flops 21889024 | bytes 1410052 | tf_op jit(solution)/shard_map/dot_general | solution.py:806
  7.5 0.0 copy-done
  7.5 1.1 copy.16
  8.5 2.2 %fusion.gained_hbm = bf16[8192,64]{1,0:T(8,128)(2,1)} fusion(bf16[1,8192,64]{2,1,0:T(8,128)(2,1)S(1)} %copy.16, f32[8192]{0:T(1024)S(1)} %bitcast.40), kind=kLoop, calls=%fused_computation.1 | loop fusion | flops 1572864 | bytes 2129920 | tf_op jit(solution)/shard_map/convert_element_type | solution.py:808
  10.7 166.4 %relay.1 = (bf16[128,8192]{1,0:T(8,128)(2,1)}, f32[80,256]{1,0:T(8,128)}) custom-call(bf16[256,512]{1,0:T(8,128)(2,1)} %fusion.3.shard, bf16[128,8192]{1,0:T(8,128)(2,1)} %hidden_hbm.1, bf16[128,8192]{1,0:T(8,128)(2,1)} %cotangent_hbm.1, bf16[8192,64]{1,0:T(8,128)(2,1)} %fusion.gained_hbm, bf16[512,64]{1,0:T(8,128)(2,1)} %bitcast.39), custom_call_target="tpu_custom_call" | custom-call | tf_op jit(solution)/shard_map/relay/pallas_call | solution.py:812
  177.2 1.3 slice_bitcast_fusion
  178.5 1.5 multiply_bitcast_fusion
  179.9 3.1 %copy.18 = bf16[1,128,8192]{2,1,0:T(8,128)(2,1)} copy(bf16[1,128,8192]{2,1,0:T(8,128)(2,1)} %bitcast.37) | data formatting | bytes 4194304
  (2 shorter events, 0.0 us)
Async XLA Ops:
  4.8 2.7 %copy-start = (bf16[1,8192,64]{1,2,0:T(8,128)(2,1)S(1)}, bf16[1,8192,64]{1,2,0:T(8,128)(2,1)}, u32[]{:S(2)}) copy-start(bf16[1,8192,64]{1,2,0:T(8,128)(2,1)} %param.12) | copy-start | bytes 3145732

commit v3 on v2

--- a/solution.py
+++ b/solution.py
@@ -38,30 +38,28 @@
 BF16 = jnp.bfloat16
 
 
-def dequantize_shard(codes, scale_codes, second_scales):
-    value_rows = jnp.zeros(codes.shape, jnp.float32)
-    for entry in range(16):
-        value_rows = jnp.where(codes == entry, jnp.float32(NF4_TABLE[entry]), value_rows)
-    outer = jnp.repeat(second_scales, SROWS)
-    block = outer[:, None] * (scale_codes.astype(jnp.float32) + 1.0) / 256.0
-    scaled = value_rows.reshape(codes.shape[0], scale_codes.shape[1], BLOCK) * block[:, :, None]
-    return scaled.reshape(codes.shape).astype(jnp.bfloat16)
-
-
 def chip_kernel(
     width,
-    shard,
+    codes_hbm,
+    scale_codes,
+    second_scales,
+    gains,
+    down_hbm,
+    raised,
     hidden_hbm,
     cotangent_hbm,
-    gained_hbm,
-    raised,
     out,
-    grad_out,
+    down_out,
+    up_out,
     weight,
     mixes,
+    codes,
+    shard,
+    quad_send,
+    quad_recv,
     hidden,
     cotangent,
-    gained,
+    down,
     product,
     product_send,
     product_recv,
@@ -76,6 +74,7 @@
     slope_send,
     scaled,
     total,
+    shifts,
     slopes,
     pair_send,
     odd,
@@ -84,11 +83,15 @@
     later,
     other_send,
     grad_send,
+    grad_mate,
+    grad_sum,
     grad_recv,
     narrow,
     local_sem,
     send_sem,
     weight_sem,
+    quad_sem,
+    depth_sem,
     mix_sem,
     product_sem,
     reply_sem,
@@ -145,9 +148,10 @@
     loads = [
         pltpu.make_async_copy(hidden_hbm, hidden, local_sem.at[0]),
         pltpu.make_async_copy(cotangent_hbm, cotangent, local_sem.at[1]),
-        pltpu.make_async_copy(gained_hbm, gained, local_sem.at[2]),
+        pltpu.make_async_copy(down_hbm, down, local_sem.at[2]),
+        pltpu.make_async_copy(codes_hbm, codes, local_sem.at[5]),
     ]
-    for load in loads:
+    for load in reversed(loads):
         load.start()
 
     barrier = pltpu.get_barrier_semaphore()
@@ -165,6 +169,32 @@
     for step in range(1, layers):
         greet(device((section + step) % 8, place))
     greet(swap)
+
+    loads[3].wait()
+    loads[2].wait()
+    own_features = pl.ds(pl.multiple_of(place * 256, 256), 256)
+    lane = lax.broadcasted_iota(jnp.int32, (8, 256), 1)
+    outer = jnp.full((8, 256), second_scales[0, 0], F32)
+    for group in range(1, 8):
+        outer = jnp.where(lane >= group * SROWS, second_scales[0, group], outer)
+    block_scale = outer * (scale_codes[...].astype(F32) + 1.0) / 256.0
+    gain_lanes = jnp.broadcast_to(gains[:, own_features].astype(F32), (120, 256))
+    columns_of = jnp.concatenate([block_scale, gain_lanes], axis=0).T
+    side = lax.broadcasted_iota(jnp.int32, (256, HEAD), 1) < BLOCK
+    low_rank = lax.dot_general(
+        down[:, own_features], raised[...], (((0,), (0,)), ((), ())), preferred_element_type=F32
+    )
+    for tile in range(KV_HEADS):
+        at = slice(tile * HEAD, (tile + 1) * HEAD)
+        entries = codes[:, at]
+        looked = jnp.full((256, HEAD), NF4_TABLE[0], F32)
+        for entry in range(1, 16):
+            looked = jnp.where(entries == entry, NF4_TABLE[entry], looked)
+        left = columns_of[:, 2 * tile : 2 * tile + 1]
+        right = columns_of[:, 2 * tile + 1 : 2 * tile + 2]
+        base = (looked * jnp.where(side, left, right)).astype(BF16).astype(F32)
+        rows_of = (base + adapter_scale * low_rank[:, at]) * columns_of[:, 8:9]
+        shard[:, at] = rows_of.astype(BF16)
     pl.semaphore_wait(barrier, 31 + 7 + 1)
 
     pending = []
@@ -200,7 +230,6 @@
 
     loads[0].wait()
     loads[1].wait()
-    loads[2].wait()
     rows = pl.ds(y * 32, 32)
 
     def fold(ref):
@@ -216,6 +245,85 @@
         pltpu.make_async_copy(shard, weight.at[place], local_sem.at[3]).wait()
 
     others = [place, slot(1 - xl, z, core)]
+
+    mix_layer = 2 * y + xl
+    quarter_at = (z % 2) * 2 + core
+    fellows = (
+        (quarter_at + 1 - 2 * core, mate),
+        ((1 - z % 2) * 2 + core, device(section, xl * 16 + (z + 1 - 2 * (z % 2)) * 2 + core)),
+        (
+            (1 - z % 2) * 2 + 1 - core,
+            device(section, xl * 16 + (z + 1 - 2 * (z % 2)) * 2 + 1 - core),
+        ),
+    )
+    early_base = used[0]
+    used[0] += 20
+    y_up, y_down = (y + 1) % 4, (y + 3) % 4
+    y_far = (y + 2) % 4
+
+    def quad_copy(index):
+        which, to = fellows[index]
+        return (
+            quad_send.at[which],
+            quad_recv.at[quarter_at],
+            quad_sem.at[quarter_at],
+            to,
+            send_sem.at[early_base + index],
+        )
+
+    def depth_copy(step):
+        rows_at = mixes.at[mix_layer, z, core]
+        to = device(section, xl * 16 + ((z + step) % 8) * 2 + core)
+        return (rows_at, rows_at, depth_sem.at[z], to, send_sem.at[early_base + 2 + step])
+
+    def mix_block(which_y, which, part=None):
+        if part is None:
+            return mixes.at[pl.ds(2 * which_y, 2), :, which]
+        return mixes.at[pl.ds(2 * which_y, 2), pl.ds(part * 4, 4), which]
+
+    mix_moves = (
+        (mix_block(y, core), 0, (2 * y_up, place)),
+        (mix_block(y, core), 1, (2 * y_down, place)),
+        (mix_block(y_down, core, 0), 2, (2 * y_up, place)),
+        (mix_block(y_up, core, 1), 3, (2 * y_down, place)),
+        (mix_block(y_down, core), 4, mate),
+        (mix_block(y_up, core), 5, mate),
+        (mix_block(y_far, core, 0), 6, mate),
+        (mix_block(y_far, core, 1), 7, mate),
+        (mixes.at[mix_layer, :, core], 8, across),
+        (mix_block(y, core), 9, mate),
+    )
+
+    def mix_copy(index):
+        block, sem, to = mix_moves[index]
+        return (block, block, mix_sem.at[sem], to, send_sem.at[early_base + 10 + index])
+
+    def quad_start():
+        own = weight[place, :128].astype(F32) + weight[place, 128:].astype(F32)
+        quad_send[...] = own.astype(BF16).reshape(4, 32, KVW)
+        for index in range(3):
+            transfer(*quad_copy(index))
+
+    def depth_start():
+        summed = quad_send[quarter_at].astype(F32)
+        for which, _ in fellows:
+            arrive(quad_recv.at[which], quad_sem.at[which])
+            summed += quad_recv[which].astype(F32)
+        mixes[mix_layer, z, core] = summed.astype(BF16)
+        for step in range(1, 8):
+            transfer(*depth_copy(step))
+
+    def across_start():
+        for step in range(1, 8):
+            at_z = (z + step) % 8
+            arrive(mixes.at[mix_layer, at_z, core], depth_sem.at[at_z])
+        transfer(*mix_copy(8))
+
+    def ring_start():
+        arrive(mixes.at[2 * y + 1 - xl, :, core], mix_sem.at[8])
+        for index in (0, 1, 9):
+            transfer(*mix_copy(index))
+
     for h in range(2):
 
         @pl.when(xl != xh)
@@ -224,6 +332,12 @@
 
         if h == 0:
             pass_on(place, h, across)
+        else:
+
+            @pl.when(xh == 0)
+            def _():
+                quad_start()
+
         for to in (above, below, mate):
             pass_on(place, h, to)
     for head, part in fold(hidden):
@@ -240,6 +354,10 @@
     await_block(others[1], 0)
     for to in (above, below, mate):
         pass_on(others[1], 0, to)
+
+    @pl.when(xh == 0)
+    def _():
+        depth_start()
 
     def at_distance(distance):
         if distance == 0:
@@ -288,6 +406,18 @@
                     pass_on(block, h, across)
         if distance == 1:
             pass_on(place, 1, across)
+        if distance == 2:
+
+            @pl.when(xh == 0)
+            def _():
+                across_start()
+
+        if distance == 3:
+
+            @pl.when(xh == 0)
+            def _():
+                ring_start()
+
         relay_across(distance - 1)
         multiply(distance - 1, core)
         if distance >= 2:
@@ -299,53 +429,7 @@
         await_mate(distance)
         multiply(distance, 1 - core)
 
-    @pl.when(xh == 0)
-    def _():
-        for pair in range(2):
-            for head in range(KV_HEADS):
-
-                def add(index, carry):
-                    block = pair * 16 + head * 4 + index
-                    return (
-                        carry
-                        + weight[block, :128].astype(F32)
-                        + weight[block, 128:].astype(F32)
-                    )
-
-                mix = lax.fori_loop(0, 4, add, jnp.zeros((HEAD, KVW), F32))
-                mixes[2 * y + pair, head * HEAD : (head + 1) * HEAD] = mix.astype(BF16)
-
     product_send[...] = product[...].astype(BF16)
-    y_up, y_down = (y + 1) % 4, (y + 3) % 4
-    y_far = (y + 2) % 4
-    mix_base = used[0]
-    used[0] += 8
-
-    def mix_block(which_y, which, part=None):
-        if part is None:
-            return mixes.at[pl.ds(2 * which_y, 2), pl.ds(which * 256, 256)]
-        return mixes.at[pl.ds(2 * which_y, 2), pl.ds(which * 256 + part * 128, 128)]
-
-    mix_moves = (
-        (mix_block(y, core), 0, (2 * y_up, place)),
-        (mix_block(y, core), 1, (2 * y_down, place)),
-        (mix_block(y_down, core, 0), 2, (2 * y_up, place)),
-        (mix_block(y_up, core, 1), 3, (2 * y_down, place)),
-        (mix_block(y_down, core), 4, mate),
-        (mix_block(y_up, core), 5, mate),
-        (mix_block(y_far, core, 0), 6, mate),
-        (mix_block(y_far, core, 1), 7, mate),
-    )
-
-    def start_mix(index):
-        block, sem, to = mix_moves[index]
-        return transfer(block, block, mix_sem.at[sem], to, send_sem.at[mix_base + index])
-
-    @pl.when(xh == 0)
-    def _():
-        start_mix(0)
-        start_mix(1)
-
     product_base = used[0]
     used[0] += 4
 
@@ -408,20 +492,21 @@
     def _():
         product_recv[section] = product_send[:, rows]
         arrive(mix_block(y_down, core), mix_sem.at[0])
-        start_mix(2)
-        start_mix(4)
+        transfer(*mix_copy(2))
+        transfer(*mix_copy(4))
         arrive(mix_block(y_up, core), mix_sem.at[1])
-        start_mix(3)
-        start_mix(5)
+        transfer(*mix_copy(3))
+        transfer(*mix_copy(5))
         arrive(mix_block(y_far, core, 0), mix_sem.at[2])
-        start_mix(6)
+        transfer(*mix_copy(6))
         arrive(mix_block(y_far, core, 1), mix_sem.at[3])
-        start_mix(7)
+        transfer(*mix_copy(7))
         arrive(product_recv.at[section + 1], product_sem.at[section + 1])
         for step in range(1, 4):
             for column in range(2):
                 sender = 2 * ((y + step) % 4) + column
                 arrive(product_recv.at[sender], product_sem.at[sender])
+        arrive(mix_block(y, 1 - core), mix_sem.at[9])
         arrive(mix_block(y_down, 1 - core), mix_sem.at[4])
         arrive(mix_block(y_up, 1 - core), mix_sem.at[5])
         arrive(mix_block(y_far, 1 - core, 0), mix_sem.at[6])
@@ -438,7 +523,9 @@
                 pair_at + 1, layer % 2
             ].astype(F32)
             if layer:
-                mixed += jnp.dot(running.astype(BF16), mixes[layer], preferred_element_type=F32)
+                mixed += jnp.dot(
+                    running.astype(BF16), mixes[layer].reshape(KVW, KVW), preferred_element_type=F32
+                )
             value = mixed * inverse
             totals[layer] = running
             values[layer] = value
@@ -457,13 +544,15 @@
             step_scaled = (direction * inverse).astype(BF16)
             scaled_send[layer] = step_scaled
             at = (layer % 2) * 64
-            slope_send[layer // 2, :, at : at + 64] = jnp.broadcast_to(slope, (32, 64))
+            slope_send[layer // 2, :, at : at + 64] = jnp.broadcast_to(slope, (32, 64)).astype(
+                BF16
+            )
             if layer:
                 direction = (
                     direction
                     + lax.dot_general(
                         step_scaled,
-                        mixes[layer],
+                        mixes[layer].reshape(KVW, KVW),
                         (((1,), (1,)), ((), ())),
                         preferred_element_type=F32,
                     )
@@ -489,18 +578,18 @@
         def _():
             arrive(total.at[:, token_rows], reply_sem.at[from_y * 3 + 2])
 
-        @pl.when(xh == 1)
-        def _():
-            arrive(total.at[1, token_rows], reply_sem.at[from_y * 3 + 2])
-
     for step in range(1, 4):
         await_reply(step)
 
     @pl.when(xh == 1)
     def _():
         await_reply(0)
-
-    column_flag = (1 - xh).astype(F32)
+        shifts[...] = jnp.zeros_like(shifts)
+
+    @pl.when(xh == 0)
+    def _():
+        shifts[...] = total[...]
+
     pair_base = used[0]
     used[0] += 28
     quarter = half_width // 4
@@ -544,11 +633,9 @@
             part = hidden[:, columns].astype(F32)
             grads = []
             for pair in range(2):
-                shift = jnp.where(
-                    xh == 0, total[pair, :, q * HEAD : (q + 1) * HEAD].astype(F32), 0.0
-                )
+                shift = shifts[pair, :, q * HEAD : (q + 1) * HEAD].astype(F32)
                 current = part + jnp.concatenate([shift, shift], axis=1)
-                slope = slopes[:, pair * 64 : pair * 64 + 1]
+                slope = slopes[:, pair * 64 : pair * 64 + 1].astype(F32)
                 grads.append(
                     lax.dot_general(
                         scaled[pair],
@@ -625,51 +712,60 @@
         lax.fori_loop(0, 4, step, 0)
         pending.append(transfer(*other_copy(q)))
 
-    def adapter_setup():
+    def await_totals():
+        for from_y in range(4):
+            arrive(total.at[1, pl.ds(from_y * 32, 32)], reply_sem.at[from_y * 3 + 2])
+
+    def adapter_low():
         low = lax.dot_general(
-            raised[...], scaled[xh], (((0,), (1,)), ((), ())), preferred_element_type=F32
+            raised[...], scaled[xh], (((1,), (1,)), ((), ())), preferred_element_type=F32
         )
         return (adapter_scale * low).astype(BF16)
 
-    def current_columns(block):
-        columns = pl.ds(pl.multiple_of(block * 256, 256), 256)
-        part = hidden[:, columns].astype(F32)
-        head = jnp.minimum(block // 4, KV_HEADS - 1)
-        shift = total[xh, :, pl.ds(pl.multiple_of(head * HEAD, HEAD), HEAD)].astype(F32)
-        shift = jnp.where(block < 16, shift, 0.0)
-        return (part + jnp.concatenate([shift, shift], axis=1)).astype(BF16)
-
-    low = adapter_setup_holder = None
-
-    def adapter_narrow(block, carry):
-        current = current_columns(block)
-        rows_at = pl.ds(pl.multiple_of(block * 256, 256), 256)
-        return carry + jnp.dot(current, gained[rows_at], preferred_element_type=F32)
-
-    def adapter_up():
-        total_narrow = lax.fori_loop(0, 32, adapter_narrow, jnp.zeros((128, 64), F32))
-        narrow[...] = total_narrow.astype(BF16)
+    def adapter_part(low, first, carry):
+        def step(block, carry):
+            columns = pl.ds(pl.multiple_of(block * 512, 512), 512)
+            part = hidden[:, columns].astype(F32)
+            if first < 8:
+                at = pl.ds(pl.multiple_of((block // 2) * HEAD, HEAD), HEAD)
+                shift = total[xh, :, at].astype(F32)
+                part += jnp.concatenate([shift, shift, shift, shift], axis=1)
+            grad = jnp.dot(low, part.astype(BF16), preferred_element_type=F32).astype(BF16)
+            grad_send[block, 0, :64] = grad[:, :256]
+            grad_send[block, 1, :64] = grad[:, 256:]
+            gained = (part * gains[:, columns].astype(F32)).astype(BF16)
+            return carry + lax.dot_general(
+                gained, down[:, columns], (((1,), (1,)), ((), ())), preferred_element_type=F32
+            )
+
+        return lax.fori_loop(first, first + 8, step, carry)
+
+    def adapter_up(carry):
+        narrow[...] = carry.astype(BF16)
         up_grad = adapter_scale * lax.dot_general(
             scaled[xh], narrow[...], (((0,), (0,)), ((), ())), preferred_element_type=F32
         )
         padded = jnp.concatenate([up_grad, jnp.zeros((KVW, 192), F32)], axis=1)
-        grad_send[:, 64:] = padded.astype(BF16).reshape(32, 16, 256)
-
-    def adapter_down(low):
-        def step(block, carry):
-            grad = jnp.dot(low, current_columns(block), preferred_element_type=F32)
-            grad_send[block, :64] = grad.astype(BF16)
-            return carry
-
-        lax.fori_loop(0, 32, step, 0)
+        grad_send[:, :, 64:] = padded.astype(BF16).reshape(16, 2, 16, 256)
+
+    def mate_copy():
+        return (
+            grad_send.at[:, 1 - core],
+            grad_mate,
+            grad_sem.at[16],
+            mate,
+            grad_send_sem.at[16],
+        )
+
+    seat = place // 2
 
     def grad_copy(step):
-        to = (place + step) % 32
+        to = (seat + step) % 16
         return (
-            grad_send.at[to],
-            grad_recv.at[place],
-            grad_sem.at[place],
-            device(section, to),
+            grad_sum.at[to],
+            grad_recv.at[seat],
+            grad_sem.at[seat],
+            device(section, 2 * to + core),
             grad_send_sem.at[step],
         )
 
@@ -681,28 +777,45 @@
         hidden_gradients(q)
     suffix(0)
     suffix(1)
-    adapter_up()
+
+    @pl.when(xh == 1)
+    def _():
+        await_totals()
+
+    low = adapter_low()
+    carry = adapter_part(low, 0, jnp.zeros((128, 64), F32))
     suffix(2)
+    suffix(3)
     finish(0)
-    suffix(3)
     finish(1)
-    adapter_down(adapter_setup())
-    lax.fori_loop(1, 32, send_grads, 0)
+    adapter_up(adapter_part(low, 8, carry))
+    transfer(*mate_copy())
     finish(2)
     finish(3)
-    grad_recv[place] = grad_send[place]
+    arrive(grad_mate, grad_sem.at[16])
+
+    def sum_mate(index, carry):
+        both = grad_send[index, core].astype(F32) + grad_mate[index].astype(F32)
+        grad_sum[index] = both.astype(BF16)
+        return carry
+
+    lax.fori_loop(0, 16, sum_mate, 0)
+    lax.fori_loop(1, 16, send_grads, 0)
+    grad_recv[seat] = grad_sum[seat]
 
     def await_grads(step, carry):
-        sender = (place + 32 - step) % 32
+        sender = (seat + 16 - step) % 16
         arrive(grad_recv.at[sender], grad_sem.at[sender])
         return carry
 
-    lax.fori_loop(1, 32, await_grads, 0)
+    lax.fori_loop(1, 16, await_grads, 0)
 
     def sum_grads(index, carry):
         return carry + grad_recv[index].astype(F32)
 
-    grad_out[...] = lax.fori_loop(0, 32, sum_grads, jnp.zeros((80, 256), F32))
+    summed = lax.fori_loop(0, 16, sum_grads, jnp.zeros((80, 256), F32))
+    down_out[...] = summed[:64] * gains[:, own_features].astype(F32)
+    up_out[...] = summed[64:, :64]
     for q in range(4):
         columns = pl.ds(
             pl.multiple_of((1 - xh) * half_width + q * quarter, quarter), quarter
@@ -738,9 +851,12 @@
 
     @pl.when(xh == 0)
     def _():
-        for index in range(8):
-            block, sem, to = mix_moves[index]
-            gone((block, block, mix_sem.at[sem], to, send_sem.at[mix_base + index]))
+        for index in range(3):
+            gone(quad_copy(index))
+        for step in range(1, 8):
+            gone(depth_copy(step))
+        for index in range(10):
+            gone(mix_copy(index))
         for step in range(4):
             for column in range(2):
                 if step or column:
@@ -776,7 +892,8 @@
         gone(grad_copy(step))
         return carry
 
-    lax.fori_loop(1, 32, grads_gone, 0)
+    lax.fori_loop(1, 16, grads_gone, 0)
+    gone(mate_copy())
     assert used[0] <= SENDS, used
 
 
@@ -793,36 +910,30 @@
     hidden_in,
     cotangent,
 ):
-    place = lax.axis_index("fsdp")
-    gain = gains[0].astype(F32)
-    down = down_adapter[0]
-    raised = up_projection_weight[0]
     tokens, width = hidden_in.shape
-    own_rows = codes.shape[1]
-
-    base = dequantize_shard(codes[0], scale_codes[0], second_scales[0])
-    down_rows = lax.dynamic_slice_in_dim(down, place * own_rows, own_rows, 0)
-    gain_rows = lax.dynamic_slice_in_dim(gain, place * own_rows, own_rows, 0)
-    low = jnp.dot(down_rows, raised.T, preferred_element_type=F32)
-    shard = ((base.astype(F32) + adapter_scale * low) * gain_rows[:, None]).astype(BF16)
-    gained = (down.astype(F32) * gain[:, None]).astype(BF16)
     vmem = pl.BlockSpec(memory_space=pltpu.VMEM)
+    smem = pl.BlockSpec(memory_space=pltpu.SMEM)
     hbm = pl.BlockSpec(memory_space=pl.ANY)
     dma = pltpu.SemaphoreType.DMA
-    input_grad, grads = pl.pallas_call(
+    input_grad, down_grad, up_grad = pl.pallas_call(
         functools.partial(chip_kernel, width),
         out_shape=(
             jax.ShapeDtypeStruct((tokens, width), BF16),
-            jax.ShapeDtypeStruct((80, 256), F32),
+            jax.ShapeDtypeStruct((64, 256), F32),
+            jax.ShapeDtypeStruct((16, 64), F32),
         ),
-        in_specs=[vmem, hbm, hbm, hbm, vmem],
-        out_specs=(vmem, vmem),
+        in_specs=[hbm, vmem, smem, vmem, hbm, vmem, hbm, hbm],
+        out_specs=(vmem, vmem, vmem),
         scratch_shapes=[
             pltpu.VMEM((32, 256, KVW), BF16),
-            pltpu.VMEM((8, KVW, KVW), BF16),
+            pltpu.VMEM((8, 8, 2, 32, KVW), BF16),
+            pltpu.VMEM((256, KVW), jnp.int32),
+            pltpu.VMEM((256, KVW), BF16),
+            pltpu.VMEM((4, 32, KVW), BF16),
+            pltpu.VMEM((4, 32, KVW), BF16),
             pltpu.VMEM((tokens, width), BF16),
             pltpu.VMEM((tokens, width), BF16),
-            pltpu.VMEM((width, 64), BF16),
+            pltpu.VMEM((64, width), BF16),
             pltpu.VMEM((2, tokens, KVW), F32),
             pltpu.VMEM((2, tokens, KVW), BF16),
             pltpu.VMEM((8, 2, 32, KVW), BF16),
@@ -834,38 +945,51 @@
             pltpu.VMEM((8, 32, HEAD), F32),
             pltpu.VMEM((8, 32, KVW), BF16),
             pltpu.VMEM((8, 32, KVW), BF16),
-            pltpu.VMEM((4, 32, HEAD), F32),
+            pltpu.VMEM((4, 32, HEAD), BF16),
             pltpu.VMEM((2, tokens, KVW), BF16),
             pltpu.VMEM((2, tokens, KVW), BF16),
-            pltpu.VMEM((tokens, HEAD), F32),
+            pltpu.VMEM((2, tokens, KVW), BF16),
+            pltpu.VMEM((tokens, HEAD), BF16),
             pltpu.VMEM((tokens, width // 2), BF16),
             pltpu.VMEM((tokens, width // 2), BF16),
             pltpu.VMEM((4, 32, width // 2), BF16),
             pltpu.VMEM((3, 32, width // 2), BF16),
             pltpu.VMEM((tokens, width // 2), BF16),
             pltpu.VMEM((tokens, width // 2), BF16),
-            pltpu.VMEM((32, 80, 256), BF16),
-            pltpu.VMEM((32, 80, 256), BF16),
+            pltpu.VMEM((16, 2, 80, 256), BF16),
+            pltpu.VMEM((16, 80, 256), BF16),
+            pltpu.VMEM((16, 80, 256), BF16),
+            pltpu.VMEM((16, 80, 256), BF16),
             pltpu.VMEM((tokens, 64), BF16),
-            dma((5,)),
+            dma((6,)),
             dma((SENDS,)),
             dma((64,)),
+            dma((4,)),
             dma((8,)),
+            dma((10,)),
             dma((8,)),
             dma((12,)),
             dma((16,)),
             dma((16,)),
             dma((4,)),
-            dma((32,)),
-            dma((32,)),
+            dma((17,)),
+            dma((17,)),
         ],
         compiler_params=pltpu.CompilerParams(
-            collective_id=0, has_side_effects=True, vmem_limit_bytes=58 * 2**20
+            collective_id=0, has_side_effects=True, vmem_limit_bytes=48 * 2**20
         ),
         name="relay",
-    )(shard, hidden_in, cotangent, gained, raised)
-    down_grad = grads[:64].T * gain_rows[:, None]
-    return (input_grad[None], down_grad[None], grads[None, 64:, :64])
+    )(
+        codes[0],
+        scale_codes[0].T,
+        second_scales,
+        gains,
+        down_adapter[0].T,
+        up_projection_weight[0].T,
+        hidden_in,
+        cotangent,
+    )
+    return (input_grad[None], down_grad.T[None], up_grad[None])
 
 
 def solution(mesh):

time: 183 us -> 158 us (0.86); the launches traced: 183 us -> 155 us
  Pallas kernels: 166 us -> 145 us
  other arithmetic: 5.18 us -> 0 us
  matrix products: 2.65 us -> 0 us
    pallas_call x1, Pallas kernels: 166 us -> 145 us  [shards(): pl.pallas_call(functools.partial(chip_kernel, width), out_shape=(jax.Shap...]
    unnamed x5 -> x17, local copies, waits for them, and re-layouts: 5.76 us -> 9.35 us
    convert_element_type x2 -> x0, other arithmetic: 3 us -> none  [the longest x1 2.21 us: shards(): gained = (down.astype(F32) * gain[:, None]).astype(BF16)]
    dot_general x1 -> x0, matrix products: 2.65 us -> none  [shards(): low = jnp.dot(down_rows, raised.T, preferred_element_type=F32)]
    broadcast_in_dim x2 -> x0, local copies, waits for them, and re-layouts: 2.02 us -> none  [the longest x1 1.3 us: shards(): return (input_grad[None], down_grad[None], grads[None, 64:, :64])]
where the time goes in v3:
time: 158 us; the launch traced here: 155 us
  Pallas kernels  145 us (92%)
  local copies, waits for them, and re-layouts  9.35 us (6%)
    pallas_call x1, Pallas kernels, shards(): pl.pallas_call(functools.partial(chip_kernel, width), out_shape=(jax.Shap...  145 us
    unnamed x17, local copies, waits for them, and re-layouts  9.35 us

profile of v3, /device:TPU:32, one launch (start us, length us, event | category | flops | bytes accessed | tf_op | source)
XLA Modules:
  0.0 155.3 jit_solution(12435125424497130763)
XLA Ops:
  0.6 0.0 copy-start
  0.6 1.6 %copy-done = bf16[128,8192]{1,0:T(8,128)(2,1)S(1)} copy-done((bf16[128,8192]{1,0:T(8,128)(2,1)S(1)}, bf16[128,8192]{1,0:T(8,128)(2,1)}, u32[]{:S(2)}) %copy-start) | copy-done | bytes 2097176
  2.2 0.0 copy-start.1
  2.2 1.2 copy-done.1
  3.5 0.0 copy-start.2
  3.5 1.0 copy-done.2
  4.5 0.0 copy-start.3
  4.5 0.8 copy-done.3
  5.3 0.0 copy-start.4
  5.3 0.8 copy-done.4
  6.1 0.0 copy-start.5
  6.1 0.7 copy-done.5
  6.8 0.0 copy-start.6
  6.8 0.7 copy-done.6
  7.4 145.3 %relay.1 = (bf16[128,8192]{1,0:T(8,128)(2,1)S(1)}, f32[64,256]{1,0:T(8,128)S(1)}, f32[16,64]{1,0:T(8,128)S(1)}) custom-call(s32[256,512]{1,0:T(8,128)S(1)} %bitcast.17, s32[8,256]{1,0:T(8,128)S(1)} %bitcast.20, f32[1,8]{1,0:T(1,128)S(1)} %copy-done.6, bf16[1,8192]{1,0:T(2,128)(2,1)S(1)} %copy-done.4, bf16[64,8192]{1,0:T(8,128)(2,1)S(1)} %bitcast.16, ...), custom_call_target="tpu_custom_call" | custom-call | tf_op jit(solution)/shard_map/relay/pallas_call | solution.py:918
  152.7 1.3 copy.14
  154.0 0.6 copy.15
  154.7 0.6 copy.16
Async XLA Ops:
  0.6 1.6 %copy-start = (bf16[128,8192]{1,0:T(8,128)(2,1)S(1)}, bf16[128,8192]{1,0:T(8,128)(2,1)}, u32[]{:S(2)}) copy-start(bf16[128,8192]{1,0:T(8,128)(2,1)} %hidden_hbm.1) | copy-start | bytes 6291460
  2.2 1.2 copy-start.1
  3.5 1.0 copy-start.2
  4.5 0.8 copy-start.3
  5.3 0.8 copy-start.4
  6.1 0.7 copy-start.5
  6.8 0.7 copy-start.6

commit v4 on v3

--- a/solution.py
+++ b/solution.py
@@ -41,11 +41,11 @@
 def chip_kernel(
     width,
     codes_hbm,
-    scale_codes,
+    scale_hbm,
     second_scales,
-    gains,
+    gains_hbm,
     down_hbm,
-    raised,
+    raised_hbm,
     hidden_hbm,
     cotangent_hbm,
     out,
@@ -54,6 +54,9 @@
     weight,
     mixes,
     codes,
+    scale_codes,
+    gains,
+    raised,
     shard,
     quad_send,
     quad_recv,
@@ -150,6 +153,9 @@
         pltpu.make_async_copy(cotangent_hbm, cotangent, local_sem.at[1]),
         pltpu.make_async_copy(down_hbm, down, local_sem.at[2]),
         pltpu.make_async_copy(codes_hbm, codes, local_sem.at[5]),
+        pltpu.make_async_copy(scale_hbm, scale_codes, local_sem.at[6]),
+        pltpu.make_async_copy(gains_hbm, gains, local_sem.at[7]),
+        pltpu.make_async_copy(raised_hbm, raised, local_sem.at[8]),
     ]
     for load in reversed(loads):
         load.start()
@@ -170,8 +176,8 @@
         greet(device((section + step) % 8, place))
     greet(swap)
 
-    loads[3].wait()
-    loads[2].wait()
+    for load in loads[2:]:
+        load.wait()
     own_features = pl.ds(pl.multiple_of(place * 256, 256), 256)
     lane = lax.broadcasted_iota(jnp.int32, (8, 256), 1)
     outer = jnp.full((8, 256), second_scales[0, 0], F32)
@@ -197,56 +203,6 @@
         shard[:, at] = rows_of.astype(BF16)
     pl.semaphore_wait(barrier, 31 + 7 + 1)
 
-    pending = []
-
-    def slot(x, depth, which):
-        return x * 16 + depth * 2 + which
-
-    def half(block, h):
-        return weight.at[block, pl.ds(h * 128, 128)]
-
-    def pass_on(block, h, to):
-        pending.append(transfer(half(block, h), half(block, h), weight_sem.at[block * 2 + h], to))
-
-    def await_block(block, h):
-        arrive(half(block, h), weight_sem.at[block * 2 + h])
-
-    swapped_place = (place + 16) % 32
-
-    @pl.when(xl != xh)
-    def _():
-        for h in range(2):
-            transfer(
-                shard.at[pl.ds(h * 128, 128)],
-                half(swapped_place, h),
-                weight_sem.at[swapped_place * 2 + h],
-                swap,
-                local_sem.at[3 + h],
-            )
-
-    @pl.when(xl == xh)
-    def _():
-        pltpu.make_async_copy(shard, weight.at[place], local_sem.at[3]).start()
-
-    loads[0].wait()
-    loads[1].wait()
-    rows = pl.ds(y * 32, 32)
-
-    def fold(ref):
-        for head in range(KV_HEADS):
-            part = jnp.zeros((32, HEAD), F32)
-            for member in range(GROUP):
-                at = (head * GROUP + member) * HEAD
-                part += ref[rows, pl.ds(at, HEAD)].astype(F32)
-            yield head, part
-
-    @pl.when(xl == xh)
-    def _():
-        pltpu.make_async_copy(shard, weight.at[place], local_sem.at[3]).wait()
-
-    others = [place, slot(1 - xl, z, core)]
-
-    mix_layer = 2 * y + xl
     quarter_at = (z % 2) * 2 + core
     fellows = (
         (quarter_at + 1 - 2 * core, mate),
@@ -257,7 +213,7 @@
         ),
     )
     early_base = used[0]
-    used[0] += 20
+    used[0] += 24
     y_up, y_down = (y + 1) % 4, (y + 3) % 4
     y_far = (y + 2) % 4
 
@@ -272,7 +228,7 @@
         )
 
     def depth_copy(step):
-        rows_at = mixes.at[mix_layer, z, core]
+        rows_at = mixes.at[section, z, core]
         to = device(section, xl * 16 + ((z + step) % 8) * 2 + core)
         return (rows_at, rows_at, depth_sem.at[z], to, send_sem.at[early_base + 2 + step])
 
@@ -282,16 +238,18 @@
         return mixes.at[pl.ds(2 * which_y, 2), pl.ds(part * 4, 4), which]
 
     mix_moves = (
-        (mix_block(y, core), 0, (2 * y_up, place)),
-        (mix_block(y, core), 1, (2 * y_down, place)),
-        (mix_block(y_down, core, 0), 2, (2 * y_up, place)),
-        (mix_block(y_up, core, 1), 3, (2 * y_down, place)),
+        (mix_block(y, core), 0, (2 * y_up + xh, place)),
+        (mix_block(y, core), 1, (2 * y_down + xh, place)),
+        (mix_block(y_down, core, 0), 2, (2 * y_up + xh, place)),
+        (mix_block(y_up, core, 1), 3, (2 * y_down + xh, place)),
         (mix_block(y_down, core), 4, mate),
         (mix_block(y_up, core), 5, mate),
         (mix_block(y_far, core, 0), 6, mate),
         (mix_block(y_far, core, 1), 7, mate),
-        (mixes.at[mix_layer, :, core], 8, across),
+        (mixes.at[section, :, core], 8, across),
         (mix_block(y, core), 9, mate),
+        (mixes.at[section, :, core], 10, swap),
+        (mixes.at[twin, :, core], 11, across),
     )
 
     def mix_copy(index):
@@ -299,7 +257,7 @@
         return (block, block, mix_sem.at[sem], to, send_sem.at[early_base + 10 + index])
 
     def quad_start():
-        own = weight[place, :128].astype(F32) + weight[place, 128:].astype(F32)
+        own = shard[:128].astype(F32) + shard[128:].astype(F32)
         quad_send[...] = own.astype(BF16).reshape(4, 32, KVW)
         for index in range(3):
             transfer(*quad_copy(index))
@@ -309,20 +267,85 @@
         for which, _ in fellows:
             arrive(quad_recv.at[which], quad_sem.at[which])
             summed += quad_recv[which].astype(F32)
-        mixes[mix_layer, z, core] = summed.astype(BF16)
+        mixes[section, z, core] = summed.astype(BF16)
         for step in range(1, 8):
             transfer(*depth_copy(step))
 
     def across_start():
-        for step in range(1, 8):
-            at_z = (z + step) % 8
-            arrive(mixes.at[mix_layer, at_z, core], depth_sem.at[at_z])
-        transfer(*mix_copy(8))
+        @pl.when(xl == 0)
+        def _():
+            for step in range(1, 8):
+                at_z = (z + step) % 8
+                arrive(mixes.at[section, at_z, core], depth_sem.at[at_z])
+            transfer(*mix_copy(8))
+            transfer(*mix_copy(10))
+
+    def across_more():
+        @pl.when(xl == 1)
+        def _():
+            arrive(mixes.at[twin, :, core], mix_sem.at[10])
+            transfer(*mix_copy(11))
+            arrive(mixes.at[section, :, core], mix_sem.at[8])
 
     def ring_start():
-        arrive(mixes.at[2 * y + 1 - xl, :, core], mix_sem.at[8])
+        @pl.when(xl == 0)
+        def _():
+            arrive(mixes.at[twin, :, core], mix_sem.at[11])
+
         for index in (0, 1, 9):
             transfer(*mix_copy(index))
+
+    @pl.when(xl == 0)
+    def _():
+        quad_start()
+
+    pending = []
+
+    def slot(x, depth, which):
+        return x * 16 + depth * 2 + which
+
+    def half(block, h):
+        return weight.at[block, pl.ds(h * 128, 128)]
+
+    def pass_on(block, h, to):
+        pending.append(transfer(half(block, h), half(block, h), weight_sem.at[block * 2 + h], to))
+
+    def await_block(block, h):
+        arrive(half(block, h), weight_sem.at[block * 2 + h])
+
+    swapped_place = (place + 16) % 32
+
+    @pl.when(xl != xh)
+    def _():
+        for h in range(2):
+            transfer(
+                shard.at[pl.ds(h * 128, 128)],
+                half(swapped_place, h),
+                weight_sem.at[swapped_place * 2 + h],
+                swap,
+                local_sem.at[3 + h],
+            )
+
+    @pl.when(xl == xh)
+    def _():
+        pltpu.make_async_copy(shard, weight.at[place], local_sem.at[3]).start()
+
+    rows = pl.ds(y * 32, 32)
+    chain_rows = pl.ds(section * 16, 16)
+
+    def fold(ref):
+        for head in range(KV_HEADS):
+            part = jnp.zeros((16, HEAD), F32)
+            for member in range(GROUP):
+                at = (head * GROUP + member) * HEAD
+                part += ref[chain_rows, pl.ds(at, HEAD)].astype(F32)
+            yield head, part
+
+    @pl.when(xl == xh)
+    def _():
+        pltpu.make_async_copy(shard, weight.at[place], local_sem.at[3]).wait()
+
+    others = [place, slot(1 - xl, z, core)]
 
     for h in range(2):
 
@@ -332,32 +355,30 @@
 
         if h == 0:
             pass_on(place, h, across)
-        else:
-
-            @pl.when(xh == 0)
-            def _():
-                quad_start()
-
         for to in (above, below, mate):
             pass_on(place, h, to)
+
+    @pl.when(xl == 0)
+    def _():
+        depth_start()
+
+    loads[0].wait()
+    loads[1].wait()
     for head, part in fold(hidden):
         folded[:, head * HEAD : (head + 1) * HEAD] = part
     for head, part in fold(cotangent):
         descent[:, head * HEAD : (head + 1) * HEAD] = part
-    square = jnp.zeros((32, HEAD), F32)
+    square = jnp.zeros((16, HEAD), F32)
     for at in range(0, width, HEAD):
-        piece = hidden[rows, pl.ds(at, HEAD)].astype(F32)
+        piece = hidden[chain_rows, pl.ds(at, HEAD)].astype(F32)
         square += piece * piece
-    squares[...] = jnp.broadcast_to(jnp.sum(square, axis=1, keepdims=True), (32, HEAD))
+    squares[...] = jnp.broadcast_to(jnp.sum(square, axis=1, keepdims=True), (16, HEAD))
     product[...] = jnp.zeros_like(product)
 
     await_block(others[1], 0)
     for to in (above, below, mate):
         pass_on(others[1], 0, to)
 
-    @pl.when(xh == 0)
-    def _():
-        depth_start()
 
     def at_distance(distance):
         if distance == 0:
@@ -393,7 +414,7 @@
 
     for distance in range(1, 5):
         low, high = (z + 8 - distance) % 8, (z + distance) % 8
-        for x, h, up_reach, down_reach in ((xl, 0, 4, 3), (1 - xl, 0, 3, 4), (xl, 1, 4, 3)):
+        for x, h, up_reach, down_reach in ((xl, 1, 3, 3), (xl, 0, 4, 3), (1 - xl, 0, 3, 4)):
             for depth, reach, onward in ((low, up_reach, above), (high, down_reach, below)):
                 if distance > reach:
                     continue
@@ -404,20 +425,21 @@
                 pass_on(block, h, mate)
                 if h == 1:
                     pass_on(block, h, across)
+            if distance == 3 and h == 1:
+                ends = slot(xl, low + (high - low) * core, core)
+                pass_on(ends, 1, device(section, xl * 16 + ((z + 1 + 6 * core) % 8) * 2 + core))
+            if distance == 4 and h == 1:
+                await_block(slot(x, low, core), 1)
+                pass_on(slot(x, low, core), 1, across)
+                pass_on(slot(x, low, core), 1, mate)
         if distance == 1:
             pass_on(place, 1, across)
+        if distance == 1:
+            across_start()
         if distance == 2:
-
-            @pl.when(xh == 0)
-            def _():
-                across_start()
-
+            across_more()
         if distance == 3:
-
-            @pl.when(xh == 0)
-            def _():
-                ring_start()
-
+            ring_start()
         relay_across(distance - 1)
         multiply(distance - 1, core)
         if distance >= 2:
@@ -430,164 +452,141 @@
         multiply(distance, 1 - core)
 
     product_send[...] = product[...].astype(BF16)
-    product_base = used[0]
-    used[0] += 4
-
-    def send_product(step):
-        to_y = (y + step) % 4
-        return transfer(
-            product_send.at[:, pl.ds(to_y * 32, 32)],
-            product_recv.at[section],
-            product_sem.at[section],
-            (2 * to_y, place),
-            send_sem.at[product_base + step],
-        )
-
-    for step in range(1, 4):
-        pending.append(send_product(step))
-
-    @pl.when(xh == 1)
-    def _():
-        send_product(0)
+    for step in range(1, 8):
+        to_section = (section + step) % 8
+        pending.append(
+            transfer(
+                product_send.at[:, pl.ds(to_section * 16, 16)],
+                product_recv.at[section],
+                product_sem.at[section],
+                (to_section, place),
+            )
+        )
 
     reply_base = used[0]
     used[0] += 24
 
-    def reply_copies(step, to_column):
-        to_y = (y + step) % 4
-        to = (2 * to_y + to_column, place)
-        at = reply_base + (step * 2 + to_column) * 3
-        yield (
-            scaled_send.at[pl.ds(2 * to_y, 2)],
-            scaled.at[:, pl.ds(y * 32, 32)],
-            reply_sem.at[y * 3],
-            to,
-            send_sem.at[at],
-        )
-        yield (
-            slope_send.at[to_y],
-            slopes.at[pl.ds(y * 32, 32)],
-            reply_sem.at[y * 3 + 1],
-            to,
-            send_sem.at[at + 1],
-        )
-        if to_column == 0:
-            yield (
-                total_send.at[pl.ds(2 * to_y, 2)],
-                total.at[:, pl.ds(y * 32, 32)],
-                reply_sem.at[y * 3 + 2],
+    def reply_copies(step):
+        to_section = (section + step) % 8
+        to = (to_section, place)
+        at = reply_base + step * 3
+        pair = pl.ds(to_section - to_section % 2, 2)
+        return (
+            (
+                scaled_send.at[pair],
+                scaled.at[:, chain_rows],
+                reply_sem.at[section * 3],
+                to,
+                send_sem.at[at],
+            ),
+            (
+                slope_send.at[to_section // 2],
+                slopes.at[chain_rows],
+                reply_sem.at[section * 3 + 1],
+                to,
+                send_sem.at[at + 1],
+            ),
+            (
+                total_send.at[pair],
+                total.at[:, chain_rows],
+                reply_sem.at[section * 3 + 2],
                 to,
                 send_sem.at[at + 2],
+            ),
+        )
+
+    product_recv[section] = product_send[:, chain_rows]
+    arrive(mix_block(y_down, core), mix_sem.at[0])
+    transfer(*mix_copy(2))
+    transfer(*mix_copy(4))
+    arrive(mix_block(y_up, core), mix_sem.at[1])
+    transfer(*mix_copy(3))
+    transfer(*mix_copy(5))
+    arrive(mix_block(y_far, core, 0), mix_sem.at[2])
+    transfer(*mix_copy(6))
+    arrive(mix_block(y_far, core, 1), mix_sem.at[3])
+    transfer(*mix_copy(7))
+    for step in range(1, 8):
+        sender = (section + step) % 8
+        arrive(product_recv.at[sender], product_sem.at[sender])
+    arrive(mix_block(y, 1 - core), mix_sem.at[9])
+    arrive(mix_block(y_down, 1 - core), mix_sem.at[4])
+    arrive(mix_block(y_up, 1 - core), mix_sem.at[5])
+    arrive(mix_block(y_far, 1 - core, 0), mix_sem.at[6])
+    arrive(mix_block(y_far, 1 - core, 1), mix_sem.at[7])
+
+    square_sum = squares[:, :1]
+    running = jnp.zeros((16, KVW), F32)
+    for layer in range(layers):
+        moved = 2.0 * folded[...] + GROUP * running
+        energy = square_sum + jnp.sum(running * moved, axis=1, keepdims=True)
+        inverse = 1.0 / jnp.sqrt(energy / width + epsilon)
+        pair_at = layer - layer % 2
+        mixed = product_recv[pair_at, layer % 2].astype(F32) + product_recv[
+            pair_at + 1, layer % 2
+        ].astype(F32)
+        if layer:
+            mixed += jnp.dot(
+                running.astype(BF16), mixes[layer].reshape(KVW, KVW), preferred_element_type=F32
             )
-        else:
-            yield (
-                total_send.at[2 * to_y + 1],
-                total.at[1, pl.ds(y * 32, 32)],
-                reply_sem.at[y * 3 + 2],
-                to,
-                send_sem.at[at + 2],
+        value = mixed * inverse
+        totals[layer] = running
+        values[layer] = value
+        inverses[layer] = jnp.broadcast_to(inverse, (16, HEAD))
+        total_send[layer] = running.astype(BF16)
+        running = running + value
+    direction = descent[...]
+    for layer in reversed(range(layers)):
+        inverse = inverses[layer][:, :1]
+        slope = (
+            jnp.sum(direction * values[layer], axis=1, keepdims=True)
+            / width
+            * inverse
+            * inverse
+        )
+        step_scaled = (direction * inverse).astype(BF16)
+        scaled_send[layer] = step_scaled
+        at = (layer % 2) * 64
+        slope_send[layer // 2, :, at : at + 64] = jnp.broadcast_to(slope, (16, 64)).astype(
+            BF16
+        )
+        if layer:
+            direction = (
+                direction
+                + lax.dot_general(
+                    step_scaled,
+                    mixes[layer].reshape(KVW, KVW),
+                    (((1,), (1,)), ((), ())),
+                    preferred_element_type=F32,
+                )
+                - (folded[...] + GROUP * totals[layer]) * slope
             )
+    for item in range(3):
+        for step in range(1, 8):
+            transfer(*reply_copies(step)[item])
+    own_pair = pl.ds(2 * y, 2)
+    scaled[:, chain_rows] = scaled_send[own_pair]
+    total[:, chain_rows] = total_send[own_pair]
+    slopes[chain_rows] = slope_send[y]
+
+    def await_totals():
+        for step in range(1, 8):
+            sender = (section + step) % 8
+            arrive(total.at[:, pl.ds(sender * 16, 16)], reply_sem.at[sender * 3 + 2])
+
+    for step in range(1, 8):
+        sender = (section + step) % 8
+        token_rows = pl.ds(sender * 16, 16)
+        arrive(scaled.at[:, token_rows], reply_sem.at[sender * 3])
+        arrive(slopes.at[token_rows], reply_sem.at[sender * 3 + 1])
+
+    @pl.when(xh == 1)
+    def _():
+        shifts[...] = jnp.zeros_like(shifts)
 
     @pl.when(xh == 0)
     def _():
-        product_recv[section] = product_send[:, rows]
-        arrive(mix_block(y_down, core), mix_sem.at[0])
-        transfer(*mix_copy(2))
-        transfer(*mix_copy(4))
-        arrive(mix_block(y_up, core), mix_sem.at[1])
-        transfer(*mix_copy(3))
-        transfer(*mix_copy(5))
-        arrive(mix_block(y_far, core, 0), mix_sem.at[2])
-        transfer(*mix_copy(6))
-        arrive(mix_block(y_far, core, 1), mix_sem.at[3])
-        transfer(*mix_copy(7))
-        arrive(product_recv.at[section + 1], product_sem.at[section + 1])
-        for step in range(1, 4):
-            for column in range(2):
-                sender = 2 * ((y + step) % 4) + column
-                arrive(product_recv.at[sender], product_sem.at[sender])
-        arrive(mix_block(y, 1 - core), mix_sem.at[9])
-        arrive(mix_block(y_down, 1 - core), mix_sem.at[4])
-        arrive(mix_block(y_up, 1 - core), mix_sem.at[5])
-        arrive(mix_block(y_far, 1 - core, 0), mix_sem.at[6])
-        arrive(mix_block(y_far, 1 - core, 1), mix_sem.at[7])
-
-        square_sum = squares[:, :1]
-        running = jnp.zeros((32, KVW), F32)
-        for layer in range(layers):
-            moved = 2.0 * folded[...] + GROUP * running
-            energy = square_sum + jnp.sum(running * moved, axis=1, keepdims=True)
-            inverse = 1.0 / jnp.sqrt(energy / width + epsilon)
-            pair_at = layer - layer % 2
-            mixed = product_recv[pair_at, layer % 2].astype(F32) + product_recv[
-                pair_at + 1, layer % 2
-            ].astype(F32)
-            if layer:
-                mixed += jnp.dot(
-                    running.astype(BF16), mixes[layer].reshape(KVW, KVW), preferred_element_type=F32
-                )
-            value = mixed * inverse
-            totals[layer] = running
-            values[layer] = value
-            inverses[layer] = jnp.broadcast_to(inverse, (32, HEAD))
-            total_send[layer] = running.astype(BF16)
-            running = running + value
-        direction = descent[...]
-        for layer in reversed(range(layers)):
-            inverse = inverses[layer][:, :1]
-            slope = (
-                jnp.sum(direction * values[layer], axis=1, keepdims=True)
-                / width
-                * inverse
-                * inverse
-            )
-            step_scaled = (direction * inverse).astype(BF16)
-            scaled_send[layer] = step_scaled
-            at = (layer % 2) * 64
-            slope_send[layer // 2, :, at : at + 64] = jnp.broadcast_to(slope, (32, 64)).astype(
-                BF16
-            )
-            if layer:
-                direction = (
-                    direction
-                    + lax.dot_general(
-                        step_scaled,
-                        mixes[layer].reshape(KVW, KVW),
-                        (((1,), (1,)), ((), ())),
-                        preferred_element_type=F32,
-                    )
-                    - (folded[...] + GROUP * totals[layer]) * slope
-                )
-        for item in range(3):
-            for step in (1, 2, 3, 0):
-                for column in range(2):
-                    if step == 0 and column == 0:
-                        continue
-                    transfer(*list(reply_copies(step, column))[item])
-        scaled[:, rows] = scaled_send[pl.ds(2 * y, 2)]
-        total[:, rows] = total_send[pl.ds(2 * y, 2)]
-        slopes[rows] = slope_send[y]
-
-    def await_reply(step):
-        from_y = (y + step) % 4
-        token_rows = pl.ds(from_y * 32, 32)
-        arrive(scaled.at[:, token_rows], reply_sem.at[from_y * 3])
-        arrive(slopes.at[token_rows], reply_sem.at[from_y * 3 + 1])
-
-        @pl.when(xh == 0)
-        def _():
-            arrive(total.at[:, token_rows], reply_sem.at[from_y * 3 + 2])
-
-    for step in range(1, 4):
-        await_reply(step)
-
-    @pl.when(xh == 1)
-    def _():
-        await_reply(0)
-        shifts[...] = jnp.zeros_like(shifts)
-
-    @pl.when(xh == 0)
-    def _():
+        await_totals()
         shifts[...] = total[...]
 
     pair_base = used[0]
@@ -712,10 +711,6 @@
         lax.fori_loop(0, 4, step, 0)
         pending.append(transfer(*other_copy(q)))
 
-    def await_totals():
-        for from_y in range(4):
-            arrive(total.at[1, pl.ds(from_y * 32, 32)], reply_sem.at[from_y * 3 + 2])
-
     def adapter_low():
         low = lax.dot_general(
             raised[...], scaled[xh], (((1,), (1,)), ((), ())), preferred_element_type=F32
@@ -776,7 +771,6 @@
     for q in range(4):
         hidden_gradients(q)
     suffix(0)
-    suffix(1)
 
     @pl.when(xh == 1)
     def _():
@@ -784,14 +778,11 @@
 
     low = adapter_low()
     carry = adapter_part(low, 0, jnp.zeros((128, 64), F32))
+    suffix(1)
+    adapter_up(adapter_part(low, 8, carry))
+    transfer(*mate_copy())
     suffix(2)
     suffix(3)
-    finish(0)
-    finish(1)
-    adapter_up(adapter_part(low, 8, carry))
-    transfer(*mate_copy())
-    finish(2)
-    finish(3)
     arrive(grad_mate, grad_sem.at[16])
 
     def sum_mate(index, carry):
@@ -802,6 +793,8 @@
     lax.fori_loop(0, 16, sum_mate, 0)
     lax.fori_loop(1, 16, send_grads, 0)
     grad_recv[seat] = grad_sum[seat]
+    for q in range(4):
+        finish(q)
 
     def await_grads(step, carry):
         sender = (seat + 16 - step) % 16
@@ -849,31 +842,24 @@
                 )
             )
 
-    @pl.when(xh == 0)
+    @pl.when(xl == 0)
     def _():
         for index in range(3):
             gone(quad_copy(index))
         for step in range(1, 8):
             gone(depth_copy(step))
-        for index in range(10):
-            gone(mix_copy(index))
-        for step in range(4):
-            for column in range(2):
-                if step or column:
-                    for copy in reply_copies(step, column):
-                        gone(copy)
-
-    @pl.when(xh == 1)
-    def _():
-        gone(
-            (
-                product_send.at[:, pl.ds(y * 32, 32)],
-                product_recv.at[section],
-                product_sem.at[section],
-                (2 * y, place),
-                send_sem.at[product_base],
-            )
-        )
+        gone(mix_copy(8))
+        gone(mix_copy(10))
+
+    @pl.when(xl == 1)
+    def _():
+        gone(mix_copy(11))
+
+    for index in (0, 1, 2, 3, 4, 5, 6, 7, 9):
+        gone(mix_copy(index))
+    for step in range(1, 8):
+        for copy in reply_copies(step):
+            gone(copy)
 
     @pl.when(y >= 1)
     def _():
@@ -913,21 +899,24 @@
     tokens, width = hidden_in.shape
     vmem = pl.BlockSpec(memory_space=pltpu.VMEM)
     smem = pl.BlockSpec(memory_space=pltpu.SMEM)
-    hbm = pl.BlockSpec(memory_space=pl.ANY)
+    hbm = pl.BlockSpec(memory_space=pltpu.HBM)
     dma = pltpu.SemaphoreType.DMA
     input_grad, down_grad, up_grad = pl.pallas_call(
         functools.partial(chip_kernel, width),
         out_shape=(
-            jax.ShapeDtypeStruct((tokens, width), BF16),
-            jax.ShapeDtypeStruct((64, 256), F32),
-            jax.ShapeDtypeStruct((16, 64), F32),
+            pltpu.VMEM((tokens, width), BF16),
+            pltpu.VMEM((64, 256), F32),
+            pltpu.VMEM((16, 64), F32),
         ),
-        in_specs=[hbm, vmem, smem, vmem, hbm, vmem, hbm, hbm],
+        in_specs=[hbm, hbm, smem, hbm, hbm, hbm, hbm, hbm],
         out_specs=(vmem, vmem, vmem),
         scratch_shapes=[
             pltpu.VMEM((32, 256, KVW), BF16),
             pltpu.VMEM((8, 8, 2, 32, KVW), BF16),
             pltpu.VMEM((256, KVW), jnp.int32),
+            pltpu.VMEM((8, 256), jnp.int32),
+            pltpu.VMEM((1, width), BF16),
+            pltpu.VMEM((64, KVW), BF16),
             pltpu.VMEM((256, KVW), BF16),
             pltpu.VMEM((4, 32, KVW), BF16),
             pltpu.VMEM((4, 32, KVW), BF16),
@@ -936,16 +925,16 @@
             pltpu.VMEM((64, width), BF16),
             pltpu.VMEM((2, tokens, KVW), F32),
             pltpu.VMEM((2, tokens, KVW), BF16),
-            pltpu.VMEM((8, 2, 32, KVW), BF16),
-            pltpu.VMEM((32, KVW), F32),
-            pltpu.VMEM((32, KVW), F32),
-            pltpu.VMEM((32, HEAD), F32),
-            pltpu.VMEM((8, 32, KVW), F32),
-            pltpu.VMEM((8, 32, KVW), F32),
-            pltpu.VMEM((8, 32, HEAD), F32),
-            pltpu.VMEM((8, 32, KVW), BF16),
-            pltpu.VMEM((8, 32, KVW), BF16),
-            pltpu.VMEM((4, 32, HEAD), BF16),
+            pltpu.VMEM((8, 2, 16, KVW), BF16),
+            pltpu.VMEM((16, KVW), F32),
+            pltpu.VMEM((16, KVW), F32),
+            pltpu.VMEM((16, HEAD), F32),
+            pltpu.VMEM((8, 16, KVW), F32),
+            pltpu.VMEM((8, 16, KVW), F32),
+            pltpu.VMEM((8, 16, HEAD), F32),
+            pltpu.VMEM((8, 16, KVW), BF16),
+            pltpu.VMEM((8, 16, KVW), BF16),
+            pltpu.VMEM((4, 16, HEAD), BF16),
             pltpu.VMEM((2, tokens, KVW), BF16),
             pltpu.VMEM((2, tokens, KVW), BF16),
             pltpu.VMEM((2, tokens, KVW), BF16),
@@ -961,14 +950,14 @@
             pltpu.VMEM((16, 80, 256), BF16),
             pltpu.VMEM((16, 80, 256), BF16),
             pltpu.VMEM((tokens, 64), BF16),
-            dma((6,)),
+            dma((9,)),
             dma((SENDS,)),
             dma((64,)),
             dma((4,)),
             dma((8,)),
-            dma((10,)),
+            dma((12,)),
             dma((8,)),
-            dma((12,)),
+            dma((24,)),
             dma((16,)),
             dma((16,)),
             dma((4,)),
@@ -976,7 +965,7 @@
             dma((17,)),
         ],
         compiler_params=pltpu.CompilerParams(
-            collective_id=0, has_side_effects=True, vmem_limit_bytes=48 * 2**20
+            collective_id=0, has_side_effects=True, vmem_limit_bytes=56 * 2**20
         ),
         name="relay",
     )(

time: 158 us -> 139 us (0.88)
  Pallas kernels: 145 us -> 133 us
  local copies, waits for them, and re-layouts: 9.35 us -> 2.55 us
    pallas_call x1, Pallas kernels: 145 us -> 133 us  [shards(): pl.pallas_call(functools.partial(chip_kernel, width), out_shape=(pltpu.VM...]
    unnamed x17 -> x3, local copies, waits for them, and re-layouts: 9.35 us -> 2.55 us
where the time goes in v4:
time: 139 us; the launch traced here: 137 us
  Pallas kernels  133 us (96%)
  local copies, waits for them, and re-layouts  2.55 us (2%)
    pallas_call x1, Pallas kernels, shards(): pl.pallas_call(functools.partial(chip_kernel, width), out_shape=(pltpu.VM...  133 us

profile of v4, /device:TPU:32, one launch (start us, length us, event | category | flops | bytes accessed | tf_op | source)
XLA Modules:
  0.0 136.5 jit_solution(15547869232428937627)
XLA Ops:
  0.6 133.3 %relay.1 = (bf16[128,8192]{1,0:T(8,128)(2,1)S(1)}, f32[64,256]{1,0:T(8,128)S(1)}, f32[16,64]{1,0:T(8,128)S(1)}) custom-call(s32[256,512]{1,0:T(8,128)} %bitcast.19, s32[8,256]{1,0:T(8,128)} %bitcast.21, f32[1,8]{1,0:T(1,128)} %second_scales.1, bf16[1,8192]{1,0:T(2,128)(2,1)} %gains_hbm.1, bf16[64,8192]{1,0:T(8,128)(2,1)} %bitcast.18, ...), custom_call_target="tpu_custom_call" | custom-call | tf_op jit(solution)/shard_map/relay/pallas_call | solution.py:904
  134.0 1.3 copy.14
  135.3 0.6 copy.15
  135.9 0.6 copy.16

commit v5 on v4

--- a/solution.py
+++ b/solution.py
@@ -295,6 +295,20 @@
         for index in (0, 1, 9):
             transfer(*mix_copy(index))
 
+    def ring_more():
+        arrive(mix_block(y_down, core), mix_sem.at[0])
+        transfer(*mix_copy(2))
+        transfer(*mix_copy(4))
+        arrive(mix_block(y_up, core), mix_sem.at[1])
+        transfer(*mix_copy(3))
+        transfer(*mix_copy(5))
+
+    def ring_last():
+        arrive(mix_block(y_far, core, 0), mix_sem.at[2])
+        transfer(*mix_copy(6))
+        arrive(mix_block(y_far, core, 1), mix_sem.at[3])
+        transfer(*mix_copy(7))
+
     @pl.when(xl == 0)
     def _():
         quad_start()
@@ -412,9 +426,17 @@
                 for h in range(2):
                     await_block(slot(x, depth, 1 - core), h)
 
+    hooks = {
+        (1, 1): across_start,
+        (1, 2): across_more,
+        (2, 1): ring_start,
+        (4, 0): ring_more,
+    }
     for distance in range(1, 5):
         low, high = (z + 8 - distance) % 8, (z + distance) % 8
-        for x, h, up_reach, down_reach in ((xl, 1, 3, 3), (xl, 0, 4, 3), (1 - xl, 0, 3, 4)):
+        for turn, (x, h, up_reach, down_reach) in enumerate(
+            ((xl, 1, 3, 3), (xl, 0, 4, 3), (1 - xl, 0, 3, 4))
+        ):
             for depth, reach, onward in ((low, up_reach, above), (high, down_reach, below)):
                 if distance > reach:
                     continue
@@ -432,20 +454,17 @@
                 await_block(slot(x, low, core), 1)
                 pass_on(slot(x, low, core), 1, across)
                 pass_on(slot(x, low, core), 1, mate)
+            if (distance, turn) in hooks:
+                hooks[distance, turn]()
         if distance == 1:
             pass_on(place, 1, across)
-        if distance == 1:
-            across_start()
-        if distance == 2:
-            across_more()
-        if distance == 3:
-            ring_start()
         relay_across(distance - 1)
         multiply(distance - 1, core)
         if distance >= 2:
             await_mate(distance - 2)
             multiply(distance - 2, 1 - core)
     relay_across(4)
+    ring_last()
     multiply(4, core)
     for distance in (3, 4):
         await_mate(distance)
@@ -465,6 +484,9 @@
 
     reply_base = used[0]
     used[0] += 24
+
+    total_base = used[0]
+    used[0] += 8
 
     def reply_copies(step):
         to_section = (section + step) % 8
@@ -486,26 +508,31 @@
                 to,
                 send_sem.at[at + 1],
             ),
-            (
-                total_send.at[pair],
-                total.at[:, chain_rows],
-                reply_sem.at[section * 3 + 2],
-                to,
-                send_sem.at[at + 2],
-            ),
-        )
+        )
+
+    def total_copy(step, column):
+        to_y = (y + step) % 4
+        if column == 0:
+            source, target = total_send.at[pl.ds(2 * to_y, 2)], total.at[:, chain_rows]
+        else:
+            source, target = total_send.at[2 * to_y + 1], total.at[1, chain_rows]
+        return (
+            source,
+            target,
+            reply_sem.at[section * 3 + 2],
+            (2 * to_y + column, place),
+            send_sem.at[total_base + step * 2 + column],
+        )
+
+    def each_total(column, act):
+        for step in range(1, 4):
+            act(total_copy(step, column))
+
+        @pl.when(xh == 1 - column)
+        def _():
+            act(total_copy(0, column))
 
     product_recv[section] = product_send[:, chain_rows]
-    arrive(mix_block(y_down, core), mix_sem.at[0])
-    transfer(*mix_copy(2))
-    transfer(*mix_copy(4))
-    arrive(mix_block(y_up, core), mix_sem.at[1])
-    transfer(*mix_copy(3))
-    transfer(*mix_copy(5))
-    arrive(mix_block(y_far, core, 0), mix_sem.at[2])
-    transfer(*mix_copy(6))
-    arrive(mix_block(y_far, core, 1), mix_sem.at[3])
-    transfer(*mix_copy(7))
     for step in range(1, 8):
         sender = (section + step) % 8
         arrive(product_recv.at[sender], product_sem.at[sender])
@@ -535,6 +562,7 @@
         inverses[layer] = jnp.broadcast_to(inverse, (16, HEAD))
         total_send[layer] = running.astype(BF16)
         running = running + value
+    each_total(0, lambda copy: transfer(*copy))
     direction = descent[...]
     for layer in reversed(range(layers)):
         inverse = inverses[layer][:, :1]
@@ -561,18 +589,19 @@
                 )
                 - (folded[...] + GROUP * totals[layer]) * slope
             )
-    for item in range(3):
+    for item in range(2):
         for step in range(1, 8):
             transfer(*reply_copies(step)[item])
+    each_total(1, lambda copy: transfer(*copy))
     own_pair = pl.ds(2 * y, 2)
     scaled[:, chain_rows] = scaled_send[own_pair]
     total[:, chain_rows] = total_send[own_pair]
     slopes[chain_rows] = slope_send[y]
 
-    def await_totals():
+    def await_totals(layers_at):
         for step in range(1, 8):
             sender = (section + step) % 8
-            arrive(total.at[:, pl.ds(sender * 16, 16)], reply_sem.at[sender * 3 + 2])
+            arrive(total.at[layers_at, pl.ds(sender * 16, 16)], reply_sem.at[sender * 3 + 2])
 
     for step in range(1, 8):
         sender = (section + step) % 8
@@ -586,7 +615,7 @@
 
     @pl.when(xh == 0)
     def _():
-        await_totals()
+        await_totals(slice(None))
         shifts[...] = total[...]
 
     pair_base = used[0]
@@ -650,6 +679,7 @@
 
         lax.fori_loop(0, 4, step, 0)
 
+    def send_pairs(q):
         @pl.when(y >= 1)
         def _():
             for step in range(1, 4):
@@ -768,33 +798,40 @@
         transfer(*grad_copy(step))
         return carry
 
-    for q in range(4):
-        hidden_gradients(q)
-    suffix(0)
-
-    @pl.when(xh == 1)
-    def _():
-        await_totals()
-
-    low = adapter_low()
-    carry = adapter_part(low, 0, jnp.zeros((128, 64), F32))
-    suffix(1)
-    adapter_up(adapter_part(low, 8, carry))
-    transfer(*mate_copy())
-    suffix(2)
-    suffix(3)
-    arrive(grad_mate, grad_sem.at[16])
-
     def sum_mate(index, carry):
         both = grad_send[index, core].astype(F32) + grad_mate[index].astype(F32)
         grad_sum[index] = both.astype(BF16)
         return carry
 
+    hidden_gradients(0)
+    send_pairs(0)
+    hidden_gradients(1)
+    send_pairs(1)
+
+    @pl.when(xh == 1)
+    def _():
+        await_totals(1)
+
+    low = adapter_low()
+    carry = adapter_part(low, 0, jnp.zeros((128, 64), F32))
+    adapter_up(adapter_part(low, 8, carry))
+    transfer(*mate_copy())
+    suffix(0)
+    hidden_gradients(2)
+    send_pairs(2)
+    suffix(1)
+    hidden_gradients(3)
+    send_pairs(3)
+    arrive(grad_mate, grad_sem.at[16])
     lax.fori_loop(0, 16, sum_mate, 0)
     lax.fori_loop(1, 16, send_grads, 0)
     grad_recv[seat] = grad_sum[seat]
-    for q in range(4):
-        finish(q)
+    finish(0)
+    suffix(2)
+    finish(1)
+    suffix(3)
+    finish(2)
+    finish(3)
 
     def await_grads(step, carry):
         sender = (seat + 16 - step) % 16
@@ -860,6 +897,8 @@
     for step in range(1, 8):
         for copy in reply_copies(step):
             gone(copy)
+    each_total(0, gone)
+    each_total(1, gone)
 
     @pl.when(y >= 1)
     def _():

time: 139 us -> 129 us (0.928); the launches traced: 137 us -> 129 us
  Pallas kernels: 133 us -> 126 us
    pallas_call x1, Pallas kernels: 133 us -> 126 us  [shards(): pl.pallas_call(functools.partial(chip_kernel, width), out_shape=(pltpu.VM...]
where the time goes in v5:
time: 129 us
  Pallas kernels  126 us (98%)
  local copies, waits for them, and re-layouts  2.55 us (2%)
    pallas_call x1, Pallas kernels, shards(): pl.pallas_call(functools.partial(chip_kernel, width), out_shape=(pltpu.VM...  126 us

profile of v5, /device:TPU:32, one launch (start us, length us, event | category | flops | bytes accessed | tf_op | source)
XLA Modules:
  0.0 129.1 jit_solution(997036932081797850)
XLA Ops:
  0.6 125.9 %relay.1 = (bf16[128,8192]{1,0:T(8,128)(2,1)S(1)}, f32[64,256]{1,0:T(8,128)S(1)}, f32[16,64]{1,0:T(8,128)S(1)}) custom-call(s32[256,512]{1,0:T(8,128)} %bitcast.19, s32[8,256]{1,0:T(8,128)} %bitcast.21, f32[1,8]{1,0:T(1,128)} %second_scales.1, bf16[1,8192]{1,0:T(2,128)(2,1)} %gains_hbm.1, bf16[64,8192]{1,0:T(8,128)(2,1)} %bitcast.18, ...), custom_call_target="tpu_custom_call" | custom-call | tf_op jit(solution)/shard_map/relay/pallas_call | solution.py:943
  126.5 1.3 %copy.14 = bf16[1,128,8192]{2,1,0:T(8,128)(2,1)} copy(bf16[1,128,8192]{2,1,0:T(8,128)(2,1)S(1)} %bitcast.15) | data formatting | bytes 4194304
  127.8 0.6 copy.15
  128.5 0.6 copy.16

commit v6 on v5

--- a/solution.py
+++ b/solution.py
@@ -89,6 +89,7 @@
     grad_mate,
     grad_sum,
     grad_recv,
+    grad_cross,
     narrow,
     local_sem,
     send_sem,
@@ -782,15 +783,13 @@
             grad_send_sem.at[16],
         )
 
-    seat = place // 2
-
     def grad_copy(step):
-        to = (seat + step) % 16
+        to = (z + step) % 8
         return (
-            grad_sum.at[to],
-            grad_recv.at[seat],
-            grad_sem.at[seat],
-            device(section, 2 * to + core),
+            grad_sum.at[:, to],
+            grad_recv.at[z],
+            grad_sem.at[z],
+            device(section, xl * 16 + to * 2 + core),
             grad_send_sem.at[step],
         )
 
@@ -798,9 +797,18 @@
         transfer(*grad_copy(step))
         return carry
 
+    def cross_copy():
+        return (
+            grad_cross.at[0],
+            grad_cross.at[1],
+            grad_sem.at[17],
+            across,
+            grad_send_sem.at[17],
+        )
+
     def sum_mate(index, carry):
         both = grad_send[index, core].astype(F32) + grad_mate[index].astype(F32)
-        grad_sum[index] = both.astype(BF16)
+        grad_sum[index // 8, index % 8] = both.astype(BF16)
         return carry
 
     hidden_gradients(0)
@@ -824,8 +832,8 @@
     send_pairs(3)
     arrive(grad_mate, grad_sem.at[16])
     lax.fori_loop(0, 16, sum_mate, 0)
-    lax.fori_loop(1, 16, send_grads, 0)
-    grad_recv[seat] = grad_sum[seat]
+    lax.fori_loop(1, 8, send_grads, 0)
+    grad_recv[z] = grad_sum[:, z]
     finish(0)
     suffix(2)
     finish(1)
@@ -834,16 +842,25 @@
     finish(3)
 
     def await_grads(step, carry):
-        sender = (seat + 16 - step) % 16
+        sender = (z + 8 - step) % 8
         arrive(grad_recv.at[sender], grad_sem.at[sender])
         return carry
 
-    lax.fori_loop(1, 16, await_grads, 0)
+    lax.fori_loop(1, 8, await_grads, 0)
 
     def sum_grads(index, carry):
-        return carry + grad_recv[index].astype(F32)
-
-    summed = lax.fori_loop(0, 16, sum_grads, jnp.zeros((80, 256), F32))
+        own, cross = carry
+        return (
+            own + grad_recv[index, xl].astype(F32),
+            cross + grad_recv[index, 1 - xl].astype(F32),
+        )
+
+    nothing = jnp.zeros((80, 256), F32)
+    summed, cross = lax.fori_loop(0, 8, sum_grads, (nothing, nothing))
+    grad_cross[0] = cross.astype(BF16)
+    transfer(*cross_copy())
+    arrive(grad_cross.at[1], grad_sem.at[17])
+    summed += grad_cross[1].astype(F32)
     down_out[...] = summed[:64] * gains[:, own_features].astype(F32)
     up_out[...] = summed[64:, :64]
     for q in range(4):
@@ -917,8 +934,9 @@
         gone(grad_copy(step))
         return carry
 
-    lax.fori_loop(1, 16, grads_gone, 0)
+    lax.fori_loop(1, 8, grads_gone, 0)
     gone(mate_copy())
+    gone(cross_copy())
     assert used[0] <= SENDS, used
 
 
@@ -986,8 +1004,9 @@
             pltpu.VMEM((tokens, width // 2), BF16),
             pltpu.VMEM((16, 2, 80, 256), BF16),
             pltpu.VMEM((16, 80, 256), BF16),
-            pltpu.VMEM((16, 80, 256), BF16),
-            pltpu.VMEM((16, 80, 256), BF16),
+            pltpu.VMEM((2, 8, 80, 256), BF16),
+            pltpu.VMEM((8, 2, 80, 256), BF16),
+            pltpu.VMEM((2, 80, 256), BF16),
             pltpu.VMEM((tokens, 64), BF16),
             dma((9,)),
             dma((SENDS,)),
@@ -1000,8 +1019,8 @@
             dma((16,)),
             dma((16,)),
             dma((4,)),
-            dma((17,)),
-            dma((17,)),
+            dma((18,)),
+            dma((18,)),
         ],
         compiler_params=pltpu.CompilerParams(
             collective_id=0, has_side_effects=True, vmem_limit_bytes=56 * 2**20

time: 129 us -> 127 us (0.984)
  Pallas kernels: 126 us -> 124 us
    pallas_call x1, Pallas kernels: 126 us -> 124 us  [shards(): pl.pallas_call(functools.partial(chip_kernel, width), out_shape=(pltpu.VM...]
where the time goes in v6:
time: 127 us
  Pallas kernels  124 us (98%)
  local copies, waits for them, and re-layouts  2.55 us (2%)
    pallas_call x1, Pallas kernels, shards(): pl.pallas_call(functools.partial(chip_kernel, width), out_shape=(pltpu.VM...  124 us
    unnamed x3, local copies, waits for them, and re-layouts  2.55 us

profile of v6, /device:TPU:32, one launch (start us, length us, event | category | flops | bytes accessed | tf_op | source)
XLA Modules:
  0.0 127.0 jit_solution(11483766412066665861)
XLA Ops:
  0.6 123.8 %relay.1 = (bf16[128,8192]{1,0:T(8,128)(2,1)S(1)}, f32[64,256]{1,0:T(8,128)S(1)}, f32[16,64]{1,0:T(8,128)S(1)}) custom-call(s32[256,512]{1,0:T(8,128)} %bitcast.19, s32[8,256]{1,0:T(8,128)} %bitcast.21, f32[1,8]{1,0:T(1,128)} %second_scales.1, bf16[1,8192]{1,0:T(2,128)(2,1)} %gains_hbm.1, bf16[64,8192]{1,0:T(8,128)(2,1)} %bitcast.18, ...), custom_call_target="tpu_custom_call" | custom-call | tf_op jit(solution)/shard_map/relay/pallas_call | solution.py:961
  124.4 1.3 %copy.14 = bf16[1,128,8192]{2,1,0:T(8,128)(2,1)} copy(bf16[1,128,8192]{2,1,0:T(8,128)(2,1)S(1)} %bitcast.15) | data formatting | bytes 4194304
  125.8 0.6 copy.15
  126.4 0.6 copy.16

commit v7 on v6

--- a/solution.py
+++ b/solution.py
@@ -368,9 +368,7 @@
         def _():
             await_block(place, h)
 
-        if h == 0:
-            pass_on(place, h, across)
-        for to in (above, below, mate):
+        for to in (across, above, below, mate):
             pass_on(place, h, to)
 
     @pl.when(xl == 0)
@@ -445,9 +443,9 @@
                 await_block(block, h)
                 if distance < reach:
                     pass_on(block, h, onward)
-                pass_on(block, h, mate)
                 if h == 1:
                     pass_on(block, h, across)
+                pass_on(block, h, mate)
             if distance == 3 and h == 1:
                 ends = slot(xl, low + (high - low) * core, core)
                 pass_on(ends, 1, device(section, xl * 16 + ((z + 1 + 6 * core) % 8) * 2 + core))
@@ -457,8 +455,6 @@
                 pass_on(slot(x, low, core), 1, mate)
             if (distance, turn) in hooks:
                 hooks[distance, turn]()
-        if distance == 1:
-            pass_on(place, 1, across)
         relay_across(distance - 1)
         multiply(distance - 1, core)
         if distance >= 2:
@@ -815,6 +811,12 @@
     send_pairs(0)
     hidden_gradients(1)
     send_pairs(1)
+    hidden_gradients(2)
+    suffix(0)
+    send_pairs(2)
+    hidden_gradients(3)
+    suffix(1)
+    send_pairs(3)
 
     @pl.when(xh == 1)
     def _():
@@ -824,19 +826,13 @@
     carry = adapter_part(low, 0, jnp.zeros((128, 64), F32))
     adapter_up(adapter_part(low, 8, carry))
     transfer(*mate_copy())
-    suffix(0)
-    hidden_gradients(2)
-    send_pairs(2)
-    suffix(1)
-    hidden_gradients(3)
-    send_pairs(3)
+    finish(0)
+    suffix(2)
+    finish(1)
     arrive(grad_mate, grad_sem.at[16])
     lax.fori_loop(0, 16, sum_mate, 0)
     lax.fori_loop(1, 8, send_grads, 0)
     grad_recv[z] = grad_sum[:, z]
-    finish(0)
-    suffix(2)
-    finish(1)
     suffix(3)
     finish(2)
     finish(3)

time: 127 us -> 123 us (0.969); the launches traced: 127 us -> 121 us
  Pallas kernels: 124 us -> 118 us
    pallas_call x1, Pallas kernels: 124 us -> 118 us  [shards(): pl.pallas_call(functools.partial(chip_kernel, width), out_shape=(pltpu.VM...]
where the time goes in v7:
time: 123 us; the launch traced here: 121 us
  Pallas kernels  118 us (96%)
  local copies, waits for them, and re-layouts  2.55 us (2%)
    pallas_call x1, Pallas kernels, shards(): pl.pallas_call(functools.partial(chip_kernel, width), out_shape=(pltpu.VM...  118 us
    unnamed x3, local copies, waits for them, and re-layouts  2.55 us

profile of v7, /device:TPU:32, one launch (start us, length us, event | category | flops | bytes accessed | tf_op | source)
XLA Modules:
  0.0 120.8 jit_solution(17461683852060895029)
XLA Ops:
  0.6 117.6 %relay.1 = (bf16[128,8192]{1,0:T(8,128)(2,1)S(1)}, f32[64,256]{1,0:T(8,128)S(1)}, f32[16,64]{1,0:T(8,128)S(1)}) custom-call(s32[256,512]{1,0:T(8,128)} %bitcast.19, s32[8,256]{1,0:T(8,128)} %bitcast.21, f32[1,8]{1,0:T(1,128)} %second_scales.1, bf16[1,8192]{1,0:T(2,128)(2,1)} %gains_hbm.1, bf16[64,8192]{1,0:T(8,128)(2,1)} %bitcast.18, ...), custom_call_target="tpu_custom_call" | custom-call | tf_op jit(solution)/shard_map/relay/pallas_call | solution.py:957
  118.3 1.3 %copy.14 = bf16[1,128,8192]{2,1,0:T(8,128)(2,1)} copy(bf16[1,128,8192]{2,1,0:T(8,128)(2,1)S(1)} %bitcast.15) | data formatting | bytes 4194304
  119.6 0.6 copy.15
  120.2 0.6 copy.16
